TPU v7x, 32 devices: a whole 2x2x4 slice. The times are simulated.
32 devices in a mesh: dp: 4 (over x, y), sp: 8 (over z, core).
Axes of the slice: x: 2, y: 2, z: 4, core: 2. Of those that a mesh axis runs over, the one named last changes fastest.
Arguments:
- x_in: bfloat16 [128, 512, 1024], P('dp', 'sp'), parts along dimension 0
- dy_out: bfloat16 [128, 512, 1024], P('dp', 'sp'), parts along dimension 0
- w_query: bfloat16 [1024, 1024], replicated
- w_key: bfloat16 [1024, 1024], replicated
- w_value: bfloat16 [1024, 1024], replicated
- w_beta: bfloat16 [1024, 8], replicated
- conv_query: bfloat16 [4, 1024], replicated
- conv_key: bfloat16 [4, 1024], replicated
- conv_value: bfloat16 [4, 1024], replicated
- w_gate: bfloat16 [1024, 1024], replicated
- norm_weight: bfloat16 [128], replicated
- w_out: bfloat16 [1024, 1024], replicated
Outputs:
- output 1: bfloat16 [128, 512, 1024], P('dp', 'sp'), parts along dimension 0
- output 2: bfloat16 [128, 512, 1024], P('dp', 'sp'), parts along dimension 0
- output 3: float32 [4096, 1024], P('dp'), parts along dimension 0
- output 4: float32 [4096, 1024], P('dp'), parts along dimension 0
- output 5: float32 [4096, 1024], P('dp'), parts along dimension 0
- output 6: float32 [4096, 8], P('dp'), parts along dimension 0
- output 7: float32 [16, 1024], P('dp'), parts along dimension 0
- output 8: float32 [16, 1024], P('dp'), parts along dimension 0
- output 9: float32 [16, 1024], P('dp'), parts along dimension 0
- output 10: float32 [4096, 1024], P('dp'), parts along dimension 0
- output 11: float32 [512], P('dp'), parts along dimension 0
- output 12: float32 [4096, 1024], P('dp'), parts along dimension 0
There are 4 independent parts. A program takes and returns all parts, laid end to end along the dimension named above; an argument that names none is the same for every part.
All inputs are finite; a program needn't handle non-finite values.
Results may differ from a plain program's by a relative error of at most 0.0180959.
Values are sent between devices in bfloat16 or wider.
A program may use at most 1 GiB of HBM per device.

v0:
```python
import functools
import jax
import jax.numpy as jnp
from jax import lax
from jax.sharding import PartitionSpec as P

HEAD_DIM = 128
BLOCK_LEN = 64
CONV_TAPS = 4
HIGHEST = lax.Precision.HIGHEST


def project(act_in, weight):
    return jnp.einsum('btd,de->bte', act_in, weight, preferred_element_type=jnp.float32)


def back_project(grad_in, weight):
    return jnp.einsum('bte,de->btd', grad_in, weight, preferred_element_type=jnp.float32)


def weight_grad(act_in, grad_in):
    return jnp.einsum('btd,bte->de', act_in, grad_in, preferred_element_type=jnp.float32)


def conv_apply(p_ext, tap_f):
    seq_len = p_ext.shape[1] - (CONV_TAPS - 1)
    conv_sum = p_ext[:, 0:seq_len].astype(jnp.float32) * tap_f[0]
    for tap_idx in range(1, CONV_TAPS):
        conv_sum = conv_sum + p_ext[:, tap_idx:tap_idx + seq_len].astype(jnp.float32) * tap_f[tap_idx]
    return conv_sum


def conv_back(d_ext, p_ext, tap_f):
    pad_len = CONV_TAPS - 1
    seq_len = d_ext.shape[1] - pad_len
    d_proj = d_ext[:, pad_len:pad_len + seq_len] * tap_f[0]
    for tap_idx in range(1, CONV_TAPS):
        begin_at = pad_len - tap_idx
        d_proj = d_proj + d_ext[:, begin_at:begin_at + seq_len] * tap_f[tap_idx]
    d_own = d_ext[:, :seq_len]
    d_taps = jnp.stack([jnp.sum(d_own * p_ext[:, tap_idx:tap_idx + seq_len].astype(jnp.float32), axis=(0, 1)) for tap_idx in range(CONV_TAPS)])
    return d_proj.astype(jnp.bfloat16), d_taps


def activate(conv_sum, normalize):
    result = jax.nn.silu(conv_sum)
    if normalize:
        shaped = result.reshape(result.shape[:-1] + (-1, HEAD_DIM))
        result = (shaped * lax.rsqrt(jnp.sum(shaped * shaped, axis=-1, keepdims=True) + 1e-6)).reshape(conv_sum.shape)
    return result.astype(jnp.bfloat16)


def post_norm(attn_out, gate_pre, norm_f):
    shaped = attn_out.astype(jnp.float32).reshape(attn_out.shape[:-1] + (-1, HEAD_DIM))
    normed = shaped * lax.rsqrt(jnp.mean(shaped * shaped, axis=-1, keepdims=True) + 1e-5) * norm_f
    return (normed.reshape(attn_out.shape) * jax.nn.silu(gate_pre.astype(jnp.float32))).astype(jnp.bfloat16)


def delta_local(queries, key_vecs, values, beta_tok):
    n_seqs, seq_len, model_dim = queries.shape
    n_heads = model_dim // HEAD_DIM
    n_blocks = seq_len // BLOCK_LEN

    def to_blocks(array_in):
        return array_in.reshape(n_seqs, n_blocks, BLOCK_LEN, n_heads, HEAD_DIM).transpose(1, 0, 3, 2, 4)

    q_blk = to_blocks(queries)
    k_blk = to_blocks(key_vecs)
    v_blk = to_blocks(values)
    b_blk = beta_tok.reshape(n_seqs, n_blocks, BLOCK_LEN, n_heads).transpose(1, 0, 3, 2).astype(jnp.float32)
    positions = jnp.arange(BLOCK_LEN)
    strict = positions[:, None] > positions[None, :]
    inclusive = positions[:, None] >= positions[None, :]
    gram_mat = jnp.einsum('nbhca,nbhsa->nbhcs', k_blk, k_blk, preferred_element_type=jnp.float32)
    system = jnp.where(strict, b_blk[..., None] * gram_mat, 0.0) + jnp.eye(BLOCK_LEN, dtype=jnp.float32)
    rhs_mat = jnp.concatenate([k_blk, v_blk], axis=-1).astype(jnp.float32) * b_blk[..., None]
    solved = lax.linalg.triangular_solve(system, rhs_mat, left_side=True, lower=True, unit_diagonal=True)
    scores = jnp.where(inclusive, jnp.einsum('nbhca,nbhsa->nbhcs', q_blk, k_blk, preferred_element_type=jnp.float32), 0.0)

    def scan_step(state_mat, block_in):
        w_n, u_n, q_n, k_n, s_n = block_in
        delta_mat = u_n - jnp.einsum('bhca,bhae->bhce', w_n, state_mat, precision=HIGHEST)
        out_n = jnp.einsum('bhca,bhae->bhce', q_n.astype(jnp.float32), state_mat, precision=HIGHEST) + jnp.einsum('bhcs,bhse->bhce', s_n, delta_mat, precision=HIGHEST)
        state_mat = state_mat + jnp.einsum('bhca,bhce->bhae', k_n.astype(jnp.float32), delta_mat, precision=HIGHEST)
        return state_mat, out_n

    init_state = jnp.zeros((n_seqs, n_heads, HEAD_DIM, HEAD_DIM), jnp.float32)
    block_outs = lax.scan(scan_step, init_state, (solved[..., :HEAD_DIM], solved[..., HEAD_DIM:], q_blk, k_blk, scores))[1]
    return block_outs.transpose(1, 0, 3, 2, 4).reshape(n_seqs, seq_len, model_dim).astype(jnp.bfloat16)


def solution(mesh):
    groups = mesh.shape['sp']
    to_next = [(source, source + 1) for source in range(groups - 1)]
    to_prev = [(source + 1, source) for source in range(groups - 1)]
    seq_spec = P('dp', 'sp', None)
    full_mat = P(None, None)
    part_mat = P('dp', None)

    def to_heads(array_in):
        return lax.all_to_all(array_in, 'sp', 2, 1, tiled=True)

    def to_tokens(array_in):
        return lax.all_to_all(array_in, 'sp', 1, 2, tiled=True)

    def local_step(x_in, dy_out, w_query, w_key, w_value, w_beta, conv_query, conv_key, conv_value, w_gate, norm_weight, w_out):
        seq_dev = x_in.shape[1]
        model_dim = x_in.shape[2]
        pad_len = CONV_TAPS - 1
        proj_weights = (w_query, w_key, w_value)
        tap_sets = [tap_arr.astype(jnp.float32) for tap_arr in (conv_query, conv_key, conv_value)]
        proj_outs = [project(x_in, weight).astype(jnp.bfloat16) for weight in proj_weights]
        tail_rows = lax.ppermute(jnp.concatenate([proj_out[:, seq_dev - pad_len:] for proj_out in proj_outs], axis=-1), 'sp', to_next)
        p_exts = []
        act_pulls = []
        head_inputs = []
        for branch in range(3):
            p_ext = jnp.concatenate([tail_rows[:, :, branch * model_dim:(branch + 1) * model_dim], proj_outs[branch]], axis=1)
            act_out, act_pull = jax.vjp(functools.partial(activate, normalize=branch < 2), conv_apply(p_ext, tap_sets[branch]))
            p_exts.append(p_ext)
            act_pulls.append(act_pull)
            head_inputs.append(to_heads(act_out))
        sig_beta = jax.nn.sigmoid(project(x_in, w_beta).astype(jnp.bfloat16).astype(jnp.float32))
        beta_heads = to_heads(sig_beta.astype(jnp.bfloat16))
        attn_heads, delta_pull = jax.vjp(delta_local, head_inputs[0], head_inputs[1], head_inputs[2], beta_heads)
        attn_out = to_tokens(attn_heads)
        gate_pre = project(x_in, w_gate).astype(jnp.bfloat16)
        hidden, post_pull = jax.vjp(post_norm, attn_out, gate_pre, norm_weight.astype(jnp.float32))
        y_out = project(hidden, w_out).astype(jnp.bfloat16)

        d_hidden = back_project(dy_out, w_out).astype(jnp.bfloat16)
        d_attn, d_gate, d_norm = post_pull(d_hidden)
        head_grads = delta_pull(to_heads(d_attn))
        d_beta = to_tokens(head_grads[3])
        d_logit = (d_beta.astype(jnp.float32) * sig_beta * (1.0 - sig_beta)).astype(jnp.bfloat16)
        dx_acc = back_project(d_gate, w_gate) + back_project(d_logit, w_beta)
        d_convs = [act_pulls[branch](to_tokens(head_grads[branch]))[0] for branch in range(3)]
        front_rows = lax.ppermute(jnp.concatenate([d_conv[:, :pad_len] for d_conv in d_convs], axis=-1), 'sp', to_prev)
        proj_grads = []
        tap_grads = []
        for branch in range(3):
            d_ext = jnp.concatenate([d_convs[branch], front_rows[:, :, branch * model_dim:(branch + 1) * model_dim]], axis=1)
            d_proj, d_taps = conv_back(d_ext, p_exts[branch], tap_sets[branch])
            dx_acc = dx_acc + back_project(d_proj, proj_weights[branch])
            proj_grads.append(weight_grad(x_in, d_proj))
            tap_grads.append(d_taps)
        summed = lax.psum((proj_grads[0], proj_grads[1], proj_grads[2], weight_grad(x_in, d_logit), tap_grads[0], tap_grads[1], tap_grads[2], weight_grad(x_in, d_gate), d_norm, weight_grad(hidden, dy_out)), 'sp')
        return (y_out, dx_acc.astype(jnp.bfloat16)) + tuple(summed)

    in_specs = (seq_spec, seq_spec) + (full_mat,) * 8 + (P(None), full_mat)
    out_specs = (seq_spec, seq_spec) + (part_mat,) * 8 + (P('dp'), part_mat)
    return jax.shard_map(local_step, mesh=mesh, in_specs=in_specs, out_specs=out_specs, check_vma=False)
```

profile of v0, /device:TPU:0, one launch (start us, length us, event | category | flops | bytes accessed | tf_op | source)
XLA Modules:
  0.0 2953.0 jit_solution(10457207358958522117)
XLA Ops:
  105.7 16.8 all-to-all-start
  159.4 56.8 %all-to-all-done = bf16[8,2,131072]{2,1,0:T(2,128)(2,1)} async-done(((bf16[8,2,131072]{2,1,0:T(2,128)(2,1)}), bf16[8,2,131072]{2,1,0:T(2,128)(2,1)}, u32[]{:S(2)}, u32[]{:S(2)}) %all-to-all-start) | async-done | bytes 4194336 | tf_op jit(solution)/shard_map/all_to_all | solution.py:101
  285.8 28.6 all-to-all-done.2
  350.9 16.3 copy.407
  367.2 14.9 add_bitcast_fusion
  382.1 527.2 %custom-call.7 = f32[8,32,1,1,64,64]{1,4,5,3,2,0:T(8,128)} custom-call(f32[8,32,1,1,64,64]{1,5,4,3,2,0:T(8,128)} %add_bitcast_fusion), custom_call_target="InvertDiagBlocksLowerTriangular" | custom-call | tf_op jit(solution)/shard_map/jvp()/triangular_solve | solution.py:77
  909.3 15.6 copy.412
  946.8 23.4 fusion.111
  1063.8 169.1 %while.46 = (s32[]{:T(128)}, f32[32,1,128,128]{3,2,0,1:T(8,128)}, bf16[8,32,1,64,128]{4,3,0,1,2:T(8,128)(2,1)}, f32[8,32,1,128,128]{4,3,1,2,0:T(8,128)}, f32[8,3...) while((s32[]{:T(128)}, f32[32,1,128,128]{3,2,0,1:T(8,128)}, ...), condition=%wide.region_3.4_spmd.clone, body=%wide.region_2.3_spmd.clone.sunk | while | flops 1412956160 | bytes 27267216 | solution.py:88
  1254.4 84.3 %all-to-all-done.4 = bf16[32,512,128]{2,0,1:T(8,128)(2,1)} async-done(((bf16[32,512,128]{2,0,1:T(8,128)(2,1)}), bf16[32,512,128]{2,0,1:T(8,128)(2,1)}, u32[]{:S(2)}, u32[]{:S(2)}) %all-to-all-start.4) | async-done | bytes 4194336 | tf_op jit(solution)/shard_map/all_to_all | solution.py:104
  1400.7 15.6 copy.434
  1429.9 64.5 %all-to-all-done.5 = bf16[8,2,131072]{2,1,0:T(2,128)(2,1)} async-done(((bf16[8,2,131072]{2,1,0:T(2,128)(2,1)}), bf16[8,2,131072]{2,1,0:T(2,128)(2,1)}, u32[]{:S(2)}, u32[]{:S(2)}) %all-to-all-start.5) | async-done | bytes 4194336 | tf_op jit(solution)/shard_map/all_to_all | solution.py:101
  1540.0 384.7 %while.47 = (s32[]{:T(128)}, f32[32,1,128,128]{2,3,0,1:T(8,128)}, f32[8,32,1,64,128]{4,3,1,2,0:T(8,128)}, f32[8,32,1,64,128]{4,3,1,2,0:T(8,128)}, bf16[8,32,1,64...) while((s32[]{:T(128)}, f32[32,1,128,128]{2,3,0,1:T(8,128)}, ...), condition=%wide.region_7.8_spmd.clone, body=%wide.region_6.7_spmd.clone.sunk | while | flops 2822504448 | bytes 38803648 | solution.py:88
  1924.8 22.0 fusion.113
  1946.8 14.0 fusion.284
  1960.8 16.3 copy.439
  2008.6 25.7 fusion.112
  2068.7 84.4 %all-to-all-done.8 = bf16[32,512,128]{2,0,1:T(8,128)(2,1)} async-done(((bf16[32,512,128]{2,0,1:T(8,128)(2,1)}), bf16[32,512,128]{2,0,1:T(8,128)(2,1)}, u32[]{:S(2)}, u32[]{:S(2)}) %all-to-all-start.8) | async-done | bytes 4194336 | tf_op jit(solution)/shard_map/all_to_all | solution.py:104
  2189.8 61.5 %all-to-all-done.9 = bf16[32,512,128]{2,0,1:T(8,128)(2,1)} async-done(((bf16[32,512,128]{2,0,1:T(8,128)(2,1)}), bf16[32,512,128]{2,0,1:T(8,128)(2,1)}, u32[]{:S(2)}, u32[]{:S(2)}) %all-to-all-start.9) | async-done | bytes 4194336 | tf_op jit(solution)/shard_map/all_to_all | solution.py:104
  2290.8 58.9 %all-to-all-done.7 = bf16[32,512,128]{2,0,1:T(8,128)(2,1)} async-done(((bf16[32,512,128]{2,0,1:T(8,128)(2,1)}), bf16[32,512,128]{2,0,1:T(8,128)(2,1)}, u32[]{:S(2)}, u32[]{:S(2)}) %all-to-all-start.7) | async-done | bytes 4194336 | tf_op jit(solution)/shard_map/all_to_all | solution.py:104
  2411.3 16.9 fusion.139
  2529.2 20.2 add_convert_fusion
  2549.4 325.5 %all-reduce.9.cloned.1.call-done = (f32[1024,1024]{0,1:T(8,128)}, f32[1024,1024]{0,1:T(8,128)}, f32[1024,1024]{0,1:T(8,128)}, f32[1024,1024]{0,1:T(8,128)}, f32[1024,1024]{1,0:T(8,128)}) async-done(((f32[1024,1024]{0,1:T(8,128)}, f32[1024,1024]{0,1:T(8,128)}, f32[1024,1024]{0,1:T(8,128)}, f32[1024,1024]{0,1:T(8,128)}, f32[1024,1024]{1,0:T(8,128)}), (f32[1024,1024]{0,1:T(8,128)}, f32[1024,1024]{0,1:T(8,128)}, ...) | async-done | bytes 20971536 | tf_op jit(solution)/shard_map/psum | solution.py:147
  2896.2 38.2 %all-reduce.7.cloned.1.call-done = (f32[1024,8]{0,1:T(8,128)}, f32[4,1024]{1,0:T(4,128)}, f32[4,1024]{1,0:T(4,128)}, f32[4,1024]{1,0:T(4,128)}, f32[128]{0:T(128)}) async-done(((f32[1024,8]{0,1:T(8,128)}, f32[4,1024]{1,0:T(4,128)}, f32[4,1024]{1,0:T(4,128)}, f32[4,1024]{1,0:T(4,128)}, f32[128]{0:T(128)}), (f32[1024,8]{0,1:T(8,128)}, f32[4,1024]{1,0:T(4,128)}, f32[4,1024]{1,0:T(4,128)}, f32[4,1024]{1,0:T(4,128)}, ...) | async-done | bytes 82448 | tf_op jit(solution)/shard_map/psum | solution.py:147
  (487 shorter events, 1388.2 us)
Async XLA Ops:
  7.2 1337.7 %copy-start = (bf16[1024,1024]{1,0:T(8,128)(2,1)S(1)}, bf16[1024,1024]{1,0:T(8,128)(2,1)}, u32[]{:S(2)}) copy-start(bf16[1024,1024]{1,0:T(8,128)(2,1)} %param.25) | copy-start | bytes 6291460
  27.2 12.1 collective-permute-start
  32.8 72.8 %all-to-all-start.1 = ((bf16[8,2,1024]{2,1,0:T(2,128)(2,1)}), bf16[8,2,1024]{2,1,0:T(2,128)(2,1)S(1)}, u32[]{:S(2)}, u32[]{:S(2)}) async-start(bf16[8,2,1024]{2,1,0:T(2,128)(2,1)} %reshape.547), calls=%async_computation.1 | async-start | bytes 65536 | tf_op jit(solution)/shard_map/all_to_all | solution.py:101
  95.1 27.4 copy-start.37
  105.7 110.5 %all-to-all-start = ((bf16[8,2,131072]{2,1,0:T(2,128)(2,1)}), bf16[8,2,131072]{2,1,0:T(2,128)(2,1)}, u32[]{:S(2)}, u32[]{:S(2)}) async-start(bf16[8,2,131072]{2,1,0:T(2,128)(2,1)} %reshape.545), calls=%async_computation | async-start | bytes 8388608 | tf_op jit(solution)/shard_map/all_to_all | solution.py:101
  148.9 71.9 %copy-start.76 = (bf16[4,1024]{1,0:T(4,128)(2,1)S(1)}, bf16[4,1024]{1,0:T(4,128)(2,1)}, u32[]{:S(2)}) copy-start(bf16[4,1024]{1,0:T(4,128)(2,1)} %param.22) | copy-start | bytes 24580
  148.9 72.0 %copy-start.36 = (bf16[32,3,1024]{2,0,1:T(8,128)(2,1)S(1)}, bf16[32,3,1024]{2,0,1:T(8,128)(2,1)}, u32[]{:S(2)}) copy-start(bf16[32,3,1024]{2,0,1:T(8,128)(2,1)} %get-tuple-element.811) | copy-start | bytes 589828
  216.2 98.3 %all-to-all-start.2 = ((bf16[8,2,131072]{2,1,0:T(2,128)(2,1)}), bf16[8,2,131072]{2,1,0:T(2,128)(2,1)}, u32[]{:S(2)}, u32[]{:S(2)}) async-start(bf16[8,2,131072]{2,1,0:T(2,128)(2,1)} %reshape.549), calls=%async_computation.2 | async-start | bytes 8388608 | tf_op jit(solution)/shard_map/all_to_all | solution.py:101
  314.4 666.7 %all-to-all-start.3 = ((bf16[8,2,131072]{2,1,0:T(2,128)(2,1)}), bf16[8,2,131072]{2,1,0:T(2,128)(2,1)}, u32[]{:S(2)}, u32[]{:S(2)}) async-start(bf16[8,2,131072]{2,1,0:T(2,128)(2,1)} %reshape.551), calls=%async_computation.3 | async-start | bytes 8388608 | tf_op jit(solution)/shard_map/all_to_all | solution.py:101
  319.5 705.2 %copy-start.40 = (pred[64,64]{1,0:T(8,128)(4,1)}, pred[64,64]{1,0:T(8,128)(4,1)S(1)}, u32[]{:S(2)}) copy-start(pred[64,64]{1,0:T(8,128)(4,1)S(1)} %iota_compare_fusion) | copy-start | bytes 12292
  319.6 47.7 %copy-start.42 = (pred[64,64]{1,0:T(8,128)(4,1)}, pred[64,64]{1,0:T(8,128)(4,1)S(1)}, u32[]{:S(2)}) copy-start(pred[64,64]{1,0:T(8,128)(4,1)S(1)} %get-tuple-element.828) | copy-start | bytes 12292
  319.6 47.7 %copy-start.45 = (pred[64,64]{1,0:T(8,128)(4,1)}, pred[64,64]{1,0:T(8,128)(4,1)S(1)}, u32[]{:S(2)}) copy-start(pred[64,64]{1,0:T(8,128)(4,1)S(1)} %get-tuple-element.829) | copy-start | bytes 12292
  319.7 627.0 %copy-start.26 = (f32[8,32,64]{2,1,0:T(8,128)}, f32[8,32,64]{2,1,0:T(8,128)S(1)}, u32[]{:S(2)}) copy-start(f32[8,32,64]{2,1,0:T(8,128)S(1)} %convert_bitcast_fusion.4) | copy-start | bytes 196612
  319.9 47.4 %copy-start.17 = (f32[8,32,64]{1,2,0:T(8,128)}, f32[8,32,64]{1,2,0:T(8,128)S(1)}, u32[]{:S(2)}) copy-start(f32[8,32,64]{1,2,0:T(8,128)S(1)} %copy.406) | copy-start | bytes 196612
  1239.9 98.8 %all-to-all-start.4 = ((bf16[32,512,128]{2,0,1:T(8,128)(2,1)}), bf16[32,512,128]{2,0,1:T(8,128)(2,1)}, u32[]{:S(2)}, u32[]{:S(2)}) async-start(bf16[32,512,128]{2,0,1:T(8,128)(2,1)} %copy.426), calls=%async_computation.4 | async-start | bytes 8388608 | tf_op jit(solution)/shard_map/all_to_all | solution.py:104
  1396.1 98.3 %all-to-all-start.5 = ((bf16[8,2,131072]{2,1,0:T(2,128)(2,1)}), bf16[8,2,131072]{2,1,0:T(2,128)(2,1)}, u32[]{:S(2)}, u32[]{:S(2)}) async-start(bf16[8,2,131072]{2,1,0:T(2,128)(2,1)} %reshape.553), calls=%async_computation.5 | async-start | bytes 8388608 | tf_op jit(solution)/shard_map/all_to_all | solution.py:101
  2054.9 98.2 %all-to-all-start.8 = ((bf16[32,512,128]{2,0,1:T(8,128)(2,1)}), bf16[32,512,128]{2,0,1:T(8,128)(2,1)}, u32[]{:S(2)}, u32[]{:S(2)}) async-start(bf16[32,512,128]{2,0,1:T(8,128)(2,1)} %copy.457), calls=%async_computation.8 | async-start | bytes 8388608 | tf_op jit(solution)/shard_map/all_to_all | solution.py:104
  2153.1 98.3 %all-to-all-start.9 = ((bf16[32,512,128]{2,0,1:T(8,128)(2,1)}), bf16[32,512,128]{2,0,1:T(8,128)(2,1)}, u32[]{:S(2)}, u32[]{:S(2)}) async-start(bf16[32,512,128]{2,0,1:T(8,128)(2,1)} %copy.463), calls=%async_computation.9 | async-start | bytes 8388608 | tf_op jit(solution)/shard_map/all_to_all | solution.py:104
  2185.1 70.9 %copy-start.33 = (f32[32,64,8]{1,2,0:T(8,128)S(1)}, f32[32,64,8]{1,2,0:T(8,128)}, u32[]{:S(2)}) copy-start(f32[32,64,8]{1,2,0:T(8,128)} %copy-done.32) | copy-start | bytes 196612
  2251.4 98.3 %all-to-all-start.7 = ((bf16[32,512,128]{2,0,1:T(8,128)(2,1)}), bf16[32,512,128]{2,0,1:T(8,128)(2,1)}, u32[]{:S(2)}, u32[]{:S(2)}) async-start(bf16[32,512,128]{2,0,1:T(8,128)(2,1)} %copy.447), calls=%async_computation.7 | async-start | bytes 8388608 | tf_op jit(solution)/shard_map/all_to_all | solution.py:104
  2256.0 618.9 %all-reduce.9.cloned.1.call-start = ((), (), s32[]{:S(2)}) async-start(), calls=%async_computation.11 | async-start | bytes 41943040 | tf_op jit(solution)/shard_map/psum | solution.py:147
  2387.0 7.5 collective-permute-start.1
  2479.7 20.7 all-to-all-start.6
  2490.8 443.7 %all-reduce.7.cloned.1.call-start = ((), (), s32[]{:S(2)}) async-start(), calls=%async_computation.10 | async-start | bytes 164864 | tf_op jit(solution)/shard_map/psum | solution.py:147
  (80 other events, 865.5 us)
Sparse Core Ops, SparseCore 0:
  2455.4 419.4 all-reduce.8
  2878.7 55.6 all-reduce.6
where the time goes:
time: 2970 us; the launch traced here: 2950 us
  waiting for transfers between devices  803 us (27%)
  other arithmetic  793 us (27%)
  matrix products  756 us (25%)
  local copies, waits for them, and re-layouts  513 us (17%)
  starting transfers between devices  71.6 us (2%)
    another operation x3, other arithmetic, delta_local(): lax.linalg.triangular_solve(system, rhs_mat, left_side=True, lower=True,...  542 us
    psum x2, waiting for transfers between devices, local_step(): lax.psum((proj_grads[0], proj_grads[1], proj_grads[2], weight_grad(x_in,...  364 us
    all_to_all x5, waiting for transfers between devices, to_tokens(): return lax.all_to_all(array_in, 'sp', 1, 2, tiled=True)  289 us
    unnamed x217, local copies, waits for them, and re-layouts  175 us
    all_to_all x5, waiting for transfers between devices, to_heads(): return lax.all_to_all(array_in, 'sp', 2, 1, tiled=True)  150 us
    dot_general x24, matrix products, scan_step(): jnp.einsum('bhca,bhae->bhce', w_n, state_mat, precision=HIGHEST)  147 us
    dot_general x24, matrix products, scan_step(): jnp.einsum('bhca,bhce->bhae', k_n.astype(jnp.float32), delta_mat, precisi...  128 us
    dot_general x24, matrix products, scan_step(): jnp.einsum('bhca,bhae->bhce', q_n.astype(jnp.float32), state_mat, precisi...  119 us
  transfers between devices with their start and end apart: 14, of which 9 were waited for; matrix products, arithmetic and copies ran while one was open for 36% of the time, Pallas kernels for 0%

commit v1 on v0

v1 whole, which is shorter than its diff:
```python
import functools
import jax
import jax.numpy as jnp
from jax import lax
from jax.experimental import pallas as pl
from jax.experimental.pallas import tpu as pltpu
from jax.sharding import PartitionSpec as P

HEAD_DIM = 128
CONV_TAPS = 4
PAD = CONV_TAPS - 1
SEND_SLOTS = 4
F32 = jnp.float32
BF16 = jnp.bfloat16
MESH = pl.DeviceIdType.MESH
VMEM_LIMIT = 60 * 1024 * 1024


def project(act_in, weight):
    return jnp.einsum('btd,de->bte', act_in, weight, preferred_element_type=F32)


def back_project(grad_in, weight):
    return jnp.einsum('bte,de->btd', grad_in, weight, preferred_element_type=F32)


def weight_grad(act_in, grad_in):
    return jnp.einsum('btd,bte->de', act_in, grad_in, preferred_element_type=F32)


def bdot(lhs, rhs, lhs_dim, rhs_dim):
    return lax.dot_general(lhs, rhs, (((lhs_dim,), (rhs_dim,)), ((0,), (0,))), preferred_element_type=F32)


def split(value):
    high = value.astype(BF16)
    return high, (value - high.astype(F32)).astype(BF16)


def dot_er(lhs, rhs, lhs_dim, rhs_dim):
    return bdot(lhs, rhs[0], lhs_dim, rhs_dim) + bdot(lhs, rhs[1], lhs_dim, rhs_dim)


def dot_re(lhs, rhs, lhs_dim, rhs_dim):
    return bdot(lhs[0], rhs, lhs_dim, rhs_dim) + bdot(lhs[1], rhs, lhs_dim, rhs_dim)


def dot_rr(lhs, rhs, lhs_dim, rhs_dim):
    return bdot(lhs[0], rhs[0], lhs_dim, rhs_dim) + (bdot(lhs[0], rhs[1], lhs_dim, rhs_dim) + bdot(lhs[1], rhs[0], lhs_dim, rhs_dim))


def block_inverse(low_mat, row_idx, col_idx):
    size = low_mat.shape[-1]
    eye = (row_idx == col_idx).astype(F32)
    low_split = split(low_mat)
    inv = eye - jnp.where(row_idx // 2 == col_idx // 2, low_mat, 0.0)
    width = 2
    while width < size:
        fresh = (row_idx // (2 * width) == col_idx // (2 * width)) & (row_idx // width != col_idx // width)
        corner = jnp.where(fresh, low_mat, 0.0).astype(BF16)
        inv_b = inv.astype(BF16)
        inv = inv - bdot(bdot(inv_b, corner, 2, 1).astype(BF16), inv_b, 2, 1)
        width *= 2
    inv_split = split(inv)
    resid = eye - inv - dot_rr(low_split, inv_split, 2, 1)
    return inv + bdot(inv_split[0], resid.astype(BF16), 2, 1)


def head_cols(head):
    return pl.ds(pl.multiple_of(head * HEAD_DIM, HEAD_DIM), HEAD_DIM)


def head_columns(array_in, n_heads):
    return jnp.concatenate([array_in[:, head:head + 1][None] for head in range(n_heads)], axis=0)


def entry_barrier(me, groups):
    barrier = pltpu.get_barrier_semaphore()
    for step in (1, groups - 1):
        pl.semaphore_signal(barrier, inc=1, device_id={'sp': lax.rem(me + step, groups)}, device_id_type=MESH)
    pl.semaphore_wait(barrier, 2)


def conv_rows(ext_ref, branch, cols, taps, seq_dev):
    total = ext_ref[branch, pl.ds(8 - PAD, seq_dev), cols] * taps[0:1]
    for tap_idx in range(1, CONV_TAPS):
        total = total + ext_ref[branch, pl.ds(8 - PAD + tap_idx, seq_dev), cols] * taps[tap_idx:tap_idx + 1]
    return total


def fill_ext(ext_ref, p_refs, tail_ref, cols, head, model_dim):
    seq_dev = p_refs[0].shape[1]
    for branch in range(3):
        tail_cols = pl.ds(pl.multiple_of(branch * model_dim + head * HEAD_DIM, HEAD_DIM), HEAD_DIM)
        ext_ref[branch, pl.ds(8 - PAD, PAD), cols] = tail_ref[0, :, tail_cols].astype(F32)
        ext_ref[branch, pl.ds(8, seq_dev), cols] = p_refs[branch][0, :, cols].astype(F32)


def forward_kernel(groups, pq_ref, pk_ref, pv_ref, tail_ref, taps_ref, logit_ref, z_ref, dh_ref, norm_ref,
                   h_ref, dz_ref, do_ref, q_ref, k_ref, t_ref, s_ref, r_ref, d_ref, dnorm_ref,
                   recv, send, ext, v_buf, o_buf, send_sem, recv_sem):
    step = pl.program_id(0)
    n_steps = pl.num_programs(0)
    me = lax.axis_index('sp')
    seq_dev = pq_ref.shape[1]
    model_dim = pq_ref.shape[2]
    n_heads = model_dim // HEAD_DIM
    slot = lax.rem(step, SEND_SLOTS)

    def hop(slot_idx, step_idx):
        return pltpu.make_async_remote_copy(
            src_ref=send.at[slot_idx], dst_ref=recv.at[step_idx], send_sem=send_sem.at[slot_idx], recv_sem=recv_sem.at[step_idx],
            device_id={'sp': lax.rem(me + 1, groups)}, device_id_type=MESH)

    @pl.when(step == 0)
    def _():
        entry_barrier(me, groups)
        dnorm_ref[...] = jnp.zeros_like(dnorm_ref)

    def act_head(head, carry):
        cols = head_cols(head)
        fill_ext(ext, (pq_ref, pk_ref, pv_ref), tail_ref, cols, head, model_dim)
        for branch in range(3):
            act = jax.nn.silu(conv_rows(ext, branch, cols, taps_ref[branch, :, cols], seq_dev))
            if branch < 2:
                act = act * lax.rsqrt(jnp.sum(act * act, axis=-1, keepdims=True) + 1e-6)
                (q_ref, k_ref)[branch][0, head] = act.astype(BF16)
            else:
                v_buf[head] = act.astype(BF16)
        return carry

    lax.fori_loop(0, n_heads, act_head, 0)

    beta = jax.nn.sigmoid(logit_ref[0].astype(F32)).astype(BF16).astype(F32)
    beta3 = head_columns(beta, n_heads)
    q_all = q_ref[0]
    k_all = k_ref[0]
    row_idx = lax.broadcasted_iota(jnp.int32, (1, seq_dev, seq_dev), 1)
    col_idx = lax.broadcasted_iota(jnp.int32, (1, seq_dev, seq_dev), 2)
    gram = bdot(k_all, k_all, 2, 2)
    t_ref[0] = block_inverse(jnp.where(row_idx > col_idx, beta3 * gram, 0.0), row_idx, col_idx)

    @pl.when(me > 0)
    def _():
        hop(slot, step).wait_recv()

    @pl.when(me == 0)
    def _():
        recv[step] = jnp.zeros(recv.shape[1:], F32)

    @pl.when((me < groups - 1) & (step >= SEND_SLOTS))
    def _():
        hop(slot, step).wait_send()

    state = recv[step]
    s_ref[0] = state
    state_split = split(state)
    resid = v_buf[...].astype(F32) - dot_er(k_all, state_split, 2, 1)
    r_ref[0] = resid
    delta = dot_rr(split(t_ref[0]), split(beta3 * resid), 2, 1)
    d_ref[0] = delta
    delta_split = split(delta)
    send[slot] = state + dot_er(k_all, delta_split, 1, 1)
    scores = jnp.where(row_idx >= col_idx, bdot(q_all, k_all, 2, 2), 0.0)
    o_buf[...] = (dot_er(q_all, state_split, 2, 1) + dot_rr(split(scores), delta_split, 2, 1)).astype(BF16).astype(F32)

    @pl.when(me < groups - 1)
    def _():
        hop(slot, step).start()

    def post_head(head, carry):
        cols = head_cols(head)
        attn = o_buf[head]
        norm_w = norm_ref[...]
        z_in = z_ref[0, :, cols].astype(F32)
        dh_in = dh_ref[0, :, cols].astype(F32)
        inv_rms = lax.rsqrt(jnp.mean(attn * attn, axis=-1, keepdims=True) + 1e-5)
        unit = attn * inv_rms
        normed = unit * norm_w
        sig = jax.nn.sigmoid(z_in)
        gate = z_in * sig
        h_ref[0, :, cols] = (normed * gate).astype(BF16)
        d_normed = dh_in * gate
        dz_ref[0, :, cols] = (dh_in * normed * (sig * (1.0 + z_in * (1.0 - sig)))).astype(BF16)
        d_unit = d_normed * norm_w
        dnorm_ref[...] += jnp.sum((d_normed * unit).reshape(seq_dev // 8, 8, HEAD_DIM), axis=0)
        do_ref[0, head] = (inv_rms * (d_unit - unit * jnp.mean(unit * d_unit, axis=-1, keepdims=True))).astype(BF16)
        return carry

    lax.fori_loop(0, n_heads, post_head, 0)

    @pl.when((me < groups - 1) & (step == n_steps - 1))
    def _():
        for back in range(min(SEND_SLOTS, recv.shape[0])):
            last = recv.shape[0] - 1 - back
            hop(last % SEND_SLOTS, last).wait_send()


def backward_kernel(groups, pq_ref, pk_ref, pv_ref, tail_ref, taps_ref, logit_ref, do_ref, q_ref, k_ref, t_ref, s_ref, r_ref, d_ref,
                    dpq_ref, dpk_ref, dpv_ref, dlogit_ref, dtaps_ref,
                    recv, send, front, front_send, ext, dext, dact, send_sem, recv_sem, fsend_sem, frecv_sem):
    step = pl.program_id(0)
    n_steps = pl.num_programs(0)
    me = lax.axis_index('sp')
    seq_dev = pq_ref.shape[1]
    model_dim = pq_ref.shape[2]
    n_heads = model_dim // HEAD_DIM
    slot = lax.rem(step, SEND_SLOTS)
    to_prev = lax.rem(me + groups - 1, groups)

    def hop(slot_idx, step_idx):
        return pltpu.make_async_remote_copy(
            src_ref=send.at[slot_idx], dst_ref=recv.at[step_idx], send_sem=send_sem.at[slot_idx], recv_sem=recv_sem.at[step_idx],
            device_id={'sp': to_prev}, device_id_type=MESH)

    def front_hop(slot_idx, step_idx):
        return pltpu.make_async_remote_copy(
            src_ref=front_send.at[slot_idx], dst_ref=front.at[step_idx], send_sem=fsend_sem.at[slot_idx], recv_sem=frecv_sem.at[step_idx],
            device_id={'sp': to_prev}, device_id_type=MESH)

    @pl.when(step == 0)
    def _():
        entry_barrier(me, groups)
        dtaps_ref[...] = jnp.zeros_like(dtaps_ref)

    sig_beta = jax.nn.sigmoid(logit_ref[0].astype(F32))
    beta3 = head_columns(sig_beta.astype(BF16).astype(F32), n_heads)
    q_all = q_ref[0]
    k_all = k_ref[0]
    d_out = do_ref[0]
    row_idx = lax.broadcasted_iota(jnp.int32, (1, seq_dev, seq_dev), 1)
    col_idx = lax.broadcasted_iota(jnp.int32, (1, seq_dev, seq_dev), 2)
    gram = bdot(k_all, k_all, 2, 2)
    scores = jnp.where(row_idx >= col_idx, bdot(q_all, k_all, 2, 2), 0.0)
    t_split = split(t_ref[0])
    delta_split = split(d_ref[0])
    state_split = split(s_ref[0])
    d_delta_own = dot_re(split(scores), d_out, 1, 1)
    state_own = bdot(q_all, d_out, 1, 1)
    d_scores = jnp.where(row_idx >= col_idx, dot_er(d_out, delta_split, 2, 2), 0.0).astype(BF16)
    dact[0] = (dot_er(d_out, state_split, 2, 2) + bdot(d_scores, k_all, 2, 1)).astype(BF16)

    @pl.when(me < groups - 1)
    def _():
        hop(slot, step).wait_recv()

    @pl.when(me == groups - 1)
    def _():
        recv[step] = jnp.zeros(recv.shape[1:], F32)
        front[step] = jnp.zeros(front.shape[1:], F32)

    @pl.when((me > 0) & (step >= SEND_SLOTS))
    def _():
        hop(slot, step).wait_send()
        front_hop(slot, step).wait_send()

    d_state = recv[step]
    d_state_split = split(d_state)
    d_delta = d_delta_own + dot_er(k_all, d_state_split, 2, 1)
    d_rhs = dot_rr(t_split, split(d_delta), 1, 1)
    d_resid = beta3 * d_rhs
    d_resid_split = split(d_resid)
    send[slot] = d_state + state_own - dot_er(k_all, d_resid_split, 1, 1)
    dact[2] = d_resid.astype(BF16)
    d_low = jnp.where(row_idx > col_idx, -dot_rr(split(d_rhs), delta_split, 2, 2), 0.0)
    d_beta = jnp.sum(d_rhs * r_ref[0], axis=-1, keepdims=True) + jnp.sum(d_low * gram, axis=-1, keepdims=True)
    d_gram = (beta3 * d_low).astype(BF16)
    d_key = dot_rr(delta_split, d_state_split, 2, 2) - dot_rr(d_resid_split, state_split, 2, 2)
    d_key = d_key + bdot(d_gram, k_all, 2, 1) + bdot(d_gram, k_all, 1, 1) + bdot(d_scores, q_all, 1, 1)
    dact[1] = d_key.astype(BF16)
    lane_idx = lax.broadcasted_iota(jnp.int32, (seq_dev, n_heads), 1)
    beta_grad = jnp.zeros((seq_dev, n_heads), F32)
    for head in range(n_heads):
        beta_grad = beta_grad + jnp.where(lane_idx == head, d_beta[head], 0.0)
    dlogit_ref[0] = (beta_grad.astype(BF16).astype(F32) * sig_beta * (1.0 - sig_beta)).astype(BF16)

    @pl.when(me > 0)
    def _():
        hop(slot, step).start()

    def act_head(head, carry):
        cols = head_cols(head)
        fill_ext(ext, (pq_ref, pk_ref, pv_ref), tail_ref, cols, head, model_dim)
        for branch in range(3):
            conv_sum = conv_rows(ext, branch, cols, taps_ref[branch, :, cols], seq_dev)
            sig = jax.nn.sigmoid(conv_sum)
            d_act = dact[branch, head].astype(F32)
            if branch < 2:
                act = conv_sum * sig
                inv_norm = lax.rsqrt(jnp.sum(act * act, axis=-1, keepdims=True) + 1e-6)
                unit = act * inv_norm
                d_act = inv_norm * (d_act - unit * jnp.sum(unit * d_act, axis=-1, keepdims=True))
            d_conv = d_act * (sig * (1.0 + conv_sum * (1.0 - sig)))
            dext[branch, pl.ds(0, seq_dev), cols] = d_conv
            front_send[slot, branch, :, cols] = d_conv[0:8]
            for tap_idx in range(CONV_TAPS):
                prod = d_conv * ext[branch, pl.ds(8 - PAD + tap_idx, seq_dev), cols]
                dtaps_ref[branch, tap_idx, :, cols] += jnp.sum(prod.reshape(seq_dev // 8, 8, HEAD_DIM), axis=0)
        return carry

    lax.fori_loop(0, n_heads, act_head, 0)

    @pl.when(me > 0)
    def _():
        front_hop(slot, step).start()

    @pl.when(me < groups - 1)
    def _():
        front_hop(slot, step).wait_recv()

    def conv_head(head, carry):
        cols = head_cols(head)
        for branch in range(3):
            taps = taps_ref[branch, :, cols]
            dext[branch, pl.ds(seq_dev, 8), cols] = front[step, branch, :, cols]
            total = dext[branch, pl.ds(PAD, seq_dev), cols] * taps[0:1]
            for tap_idx in range(1, CONV_TAPS):
                total = total + dext[branch, pl.ds(PAD - tap_idx, seq_dev), cols] * taps[tap_idx:tap_idx + 1]
            (dpq_ref, dpk_ref, dpv_ref)[branch][0, :, cols] = total.astype(BF16)
        return carry

    lax.fori_loop(0, n_heads, conv_head, 0)

    @pl.when((me > 0) & (step == n_steps - 1))
    def _():
        for back in range(min(SEND_SLOTS, recv.shape[0])):
            last = recv.shape[0] - 1 - back
            hop(last % SEND_SLOTS, last).wait_send()
            front_hop(last % SEND_SLOTS, last).wait_send()


def seq_block(shape):
    return pl.BlockSpec((1,) + tuple(shape[1:]), lambda step: (step,) + (0,) * (len(shape) - 1))


def whole_block(shape):
    return pl.BlockSpec(tuple(shape), lambda step: (0,) * len(shape))


def run_forward(groups, projs, tails, taps, logits, gate_pre, d_hidden, norm_f):
    n_seqs, seq_dev, model_dim = gate_pre.shape
    n_heads = model_dim // HEAD_DIM
    tok = jax.ShapeDtypeStruct((n_seqs, seq_dev, model_dim), BF16)
    per_head_b = jax.ShapeDtypeStruct((n_seqs, n_heads, seq_dev, HEAD_DIM), BF16)
    per_head_f = jax.ShapeDtypeStruct((n_seqs, n_heads, seq_dev, HEAD_DIM), F32)
    outs = [tok, tok, per_head_b, per_head_b, per_head_b,
            jax.ShapeDtypeStruct((n_seqs, n_heads, seq_dev, seq_dev), F32),
            jax.ShapeDtypeStruct((n_seqs, n_heads, HEAD_DIM, HEAD_DIM), F32),
            per_head_f, per_head_f, jax.ShapeDtypeStruct((8, HEAD_DIM), F32)]
    ins = [*projs, tails, taps, logits, gate_pre, d_hidden, norm_f]
    return pl.pallas_call(
        functools.partial(forward_kernel, groups),
        grid=(n_seqs,),
        out_shape=outs,
        in_specs=[seq_block(arr.shape) for arr in ins[:4]] + [whole_block(taps.shape)] + [seq_block(arr.shape) for arr in ins[5:8]] + [whole_block(norm_f.shape)],
        out_specs=[seq_block(out.shape) for out in outs[:-1]] + [whole_block(outs[-1].shape)],
        scratch_shapes=[
            pltpu.VMEM((n_seqs, n_heads, HEAD_DIM, HEAD_DIM), F32),
            pltpu.VMEM((SEND_SLOTS, n_heads, HEAD_DIM, HEAD_DIM), F32),
            pltpu.VMEM((3, seq_dev + 8, model_dim), F32),
            pltpu.VMEM((n_heads, seq_dev, HEAD_DIM), BF16),
            pltpu.VMEM((n_heads, seq_dev, HEAD_DIM), F32),
            pltpu.SemaphoreType.DMA((SEND_SLOTS,)),
            pltpu.SemaphoreType.DMA((n_seqs,)),
        ],
        compiler_params=pltpu.CompilerParams(collective_id=0, has_side_effects=True, vmem_limit_bytes=VMEM_LIMIT, dimension_semantics=('arbitrary',)),
        cost_estimate=pl.CostEstimate(flops=200_000_000_000, bytes_accessed=120_000_000, transcendentals=0),
        name='delta_forward',
    )(*ins)


def run_backward(groups, projs, tails, taps, logits, d_attn, q_act, k_act, t_mat, s_mat, r_mat, d_mat):
    n_seqs, seq_dev, model_dim = projs[0].shape
    n_heads = model_dim // HEAD_DIM
    tok = jax.ShapeDtypeStruct((n_seqs, seq_dev, model_dim), BF16)
    outs = [tok, tok, tok, jax.ShapeDtypeStruct(logits.shape, BF16), jax.ShapeDtypeStruct((3, CONV_TAPS, 8, model_dim), F32)]
    ins = [*projs, tails, taps, logits, d_attn, q_act, k_act, t_mat, s_mat, r_mat, d_mat]
    return pl.pallas_call(
        functools.partial(backward_kernel, groups),
        grid=(n_seqs,),
        out_shape=outs,
        in_specs=[seq_block(arr.shape) for arr in ins[:4]] + [whole_block(taps.shape)] + [seq_block(arr.shape) for arr in ins[5:]],
        out_specs=[seq_block(out.shape) for out in outs[:-1]] + [whole_block(outs[-1].shape)],
        scratch_shapes=[
            pltpu.VMEM((n_seqs, n_heads, HEAD_DIM, HEAD_DIM), F32),
            pltpu.VMEM((SEND_SLOTS, n_heads, HEAD_DIM, HEAD_DIM), F32),
            pltpu.VMEM((n_seqs, 3, 8, model_dim), F32),
            pltpu.VMEM((SEND_SLOTS, 3, 8, model_dim), F32),
            pltpu.VMEM((3, seq_dev + 8, model_dim), F32),
            pltpu.VMEM((3, seq_dev + 8, model_dim), F32),
            pltpu.VMEM((3, n_heads, seq_dev, HEAD_DIM), BF16),
            pltpu.SemaphoreType.DMA((SEND_SLOTS,)),
            pltpu.SemaphoreType.DMA((n_seqs,)),
            pltpu.SemaphoreType.DMA((SEND_SLOTS,)),
            pltpu.SemaphoreType.DMA((n_seqs,)),
        ],
        compiler_params=pltpu.CompilerParams(collective_id=1, has_side_effects=True, vmem_limit_bytes=VMEM_LIMIT, dimension_semantics=('arbitrary',)),
        cost_estimate=pl.CostEstimate(flops=250_000_000_000, bytes_accessed=120_000_000, transcendentals=0),
        name='delta_backward',
    )(*ins)


def solution(mesh):
    groups = mesh.shape['sp']
    to_next = [(source, source + 1) for source in range(groups - 1)]
    seq_spec = P('dp', 'sp', None)
    full_mat = P(None, None)
    part_mat = P('dp', None)

    def local_step(x_in, dy_out, w_query, w_key, w_value, w_beta, conv_query, conv_key, conv_value, w_gate, norm_weight, w_out):
        seq_dev = x_in.shape[1]
        projs = [project(x_in, weight).astype(BF16) for weight in (w_query, w_key, w_value)]
        tails = lax.ppermute(jnp.concatenate([proj[:, seq_dev - PAD:] for proj in projs], axis=-1), 'sp', to_next)
        taps = jnp.stack([conv_query, conv_key, conv_value]).astype(F32)
        logits = project(x_in, w_beta).astype(BF16)
        gate_pre = project(x_in, w_gate).astype(BF16)
        d_hidden = back_project(dy_out, w_out).astype(BF16)
        norm_f = norm_weight.astype(F32).reshape(1, HEAD_DIM)
        hidden, d_gate, d_attn, q_act, k_act, t_mat, s_mat, r_mat, d_mat, dnorm = run_forward(groups, projs, tails, taps, logits, gate_pre, d_hidden, norm_f)
        y_out = project(hidden, w_out).astype(BF16)
        early = lax.psum((weight_grad(x_in, d_gate), weight_grad(hidden, dy_out)), 'sp')
        dp_q, dp_k, dp_v, d_logit, dtaps = run_backward(groups, projs, tails, taps, logits, d_attn, q_act, k_act, t_mat, s_mat, r_mat, d_mat)
        dtaps = jnp.sum(dtaps, axis=2)
        late_parts = (weight_grad(x_in, dp_q), weight_grad(x_in, dp_k), weight_grad(x_in, dp_v), weight_grad(x_in, d_logit), dtaps, jnp.sum(dnorm, axis=0))
        late_parts, early = lax.optimization_barrier((late_parts, early))
        late = lax.psum(late_parts, 'sp')
        dx_acc = back_project(d_gate, w_gate) + back_project(d_logit, w_beta) + back_project(dp_q, w_query) + back_project(dp_k, w_key) + back_project(dp_v, w_value)
        return (y_out, dx_acc.astype(BF16), late[0], late[1], late[2], late[3], late[4][0], late[4][1], late[4][2], early[0], late[5], early[1])

    in_specs = (seq_spec, seq_spec) + (full_mat,) * 8 + (P(None), full_mat)
    out_specs = (seq_spec, seq_spec) + (part_mat,) * 8 + (P('dp'), part_mat)
    return jax.shard_map(local_step, mesh=mesh, in_specs=in_specs, out_specs=out_specs, check_vma=False)
```

time: 2970 us -> 1090 us (0.37)
  other arithmetic: 793 us -> 2.74 us
  Pallas kernels: 0 us -> 644 us
  matrix products: 756 us -> 131 us
  waiting for transfers between devices: 803 us -> 250 us
  local copies, waits for them, and re-layouts: 513 us -> 34.2 us
  starting transfers between devices: 71.6 us -> 3.14 us
    pallas_call x0 -> x2, Pallas kernels: none -> 644 us  [the longest x1 453 us: run_backward(): pl.pallas_call(functools.partial(backward_kernel, groups), grid=(n_seqs,)...]
    dot_general x121 -> x18, matrix products: 693 us -> 131 us  [the longest x6 54.4 us: back_project(): jnp.einsum('bte,de->btd', grad_in, weight, preferred_element_type=F32)]
    another operation x7 -> x0, other arithmetic: 544 us -> none  [the longest x3 542 us: delta_local(): lax.linalg.triangular_solve(system, rhs_mat, left_side=True, lower=True,...]
    all_to_all x10 -> x0, waiting for transfers between devices: 439 us -> none  [the longest x5 289 us: to_tokens(): return lax.all_to_all(array_in, 'sp', 1, 2, tiled=True)]
    unnamed x217 -> x69, local copies, waits for them, and re-layouts: 175 us -> 30.8 us
    psum x2 -> x3, waiting for transfers between devices: 364 us -> 250 us  [the longest x2 250 us: local_step(): late = lax.psum(late_parts, 'sp')]
    another operation x10 -> x0, local copies, waits for them, and re-layouts: 73.6 us -> none
    reduce_sum x10 -> x2, other arithmetic: 70.6 us -> 1.25 us  [the longest x1 0.72 us: local_step(): dtaps = jnp.sum(dtaps, axis=2)]
  transfers between devices with their start and end apart: 14 -> 4, of which waited for: 9 -> 1; matrix products, arithmetic and copies ran while one was open for 36% -> 10% of each run, Pallas kernels for 0% -> 42%
where the time goes in v1:
time: 1090 us; the launch traced here: 1080 us
  Pallas kernels  644 us (59%)
  waiting for transfers between devices  250 us (23%)
  matrix products  131 us (12%)
  local copies, waits for them, and re-layouts  34.2 us (3%)
  between operations  14.5 us (1%)
    pallas_call x1, Pallas kernels, run_backward(): pl.pallas_call(functools.partial(backward_kernel, groups), grid=(n_seqs,)...  453 us
    psum x2, waiting for transfers between devices, local_step(): late = lax.psum(late_parts, 'sp')  250 us
    pallas_call x1, Pallas kernels, run_forward(): pl.pallas_call(functools.partial(forward_kernel, groups), grid=(n_seqs,),...  192 us
    dot_general x6, matrix products, back_project(): jnp.einsum('bte,de->btd', grad_in, weight, preferred_element_type=F32)  54.4 us
    dot_general x6, matrix products, weight_grad(): jnp.einsum('btd,bte->de', act_in, grad_in, preferred_element_type=F32)  46.3 us
    unnamed x69, local copies, waits for them, and re-layouts  30.8 us
    dot_general x6, matrix products, project(): return jnp.einsum('btd,de->bte', act_in, weight, preferred_element_type=F32)  30.7 us
  transfers between devices with their start and end apart: 4, of which 1 were waited for; matrix products, arithmetic and copies ran while one was open for 10% of the time, Pallas kernels for 42%

profile of v1, /device:TPU:0, one launch (start us, length us, event | category | flops | bytes accessed | tf_op | source)
XLA Modules:
  0.0 1080.0 jit_solution(5101031439059070645)
XLA Ops:
  8.8 7.1 convolution_convert_fusion.5.pq_ref
  16.0 4.8 convolution_convert_fusion.4.pk_ref
  21.0 4.8 convolution_convert_fusion.3.pv_ref
  31.4 6.0 convolution_convert_fusion.2.z_ref
  37.5 6.1 convolution_convert_fusion.1.dh_ref
  48.3 191.7 %delta_forward.1 = (bf16[32,64,1024]{2,1,0:T(8,128)(2,1)}, bf16[32,64,1024]{2,1,0:T(8,128)(2,1)}, bf16[32,8,64,128]{3,2,1,0:T(8,128)(2,1)}, bf16[32,8,64,128]{3,...) custom-call(bf16[32,64,1024]{2,1,0:T(8,128)(2,1)} %copy-done.11, ...), custom_call_target="tpu_custom_call" | custom-call | flops 199999995904 | bytes 120000000 | tf_op jit(solution)/shard_map/delta_forward/pallas_call | solution.py:351
  240.1 10.2 convolution_bitcast_fusion
  250.2 6.1 convolution_bitcast_fusion.1
  256.4 452.5 %delta_backward.1 = (bf16[32,64,1024]{2,1,0:T(8,128)(2,1)}, bf16[32,64,1024]{2,1,0:T(8,128)(2,1)}, bf16[32,64,1024]{2,1,0:T(8,128)(2,1)}, bf16[32,64,8]{2,1,0:T(8,128)(2,1)}, f32[3,4,8,1024]{3,2,1,0:T(8,128)}) custom-call(bf16[32,64,1024]{2,1,0:T(8,128)(2,1)} %copy-done.11, bf16[32,64,1024]{2,1,0:T(8,128)(2,1)} %copy-done.12, ...), custom_call_target="tpu_custom_call" | custom-call | flops 249999998976 | bytes 120000000 | tf_op jit(solution)/shard_map/delta_backward/pallas_call | solution.py:378
  709.0 10.1 convolution_bitcast_fusion.4
  723.8 10.2 convolution_bitcast_fusion.3
  734.0 6.3 convolution_bitcast_fusion.2
  740.4 4.5 fusion.16
  744.9 9.1 fusion.13
  754.1 7.2 fusion.10
  761.3 6.0 convolution_convert_fusion
  767.4 7.3 fusion.2
  774.7 20.1 %add_convert_fusion = bf16[32,64,1024]{2,1,0:T(8,128)(2,1)} fusion(f32[32,64,1024]{2,1,0:T(8,128)} %fusion.10, f32[32,64,1024]{2,1,0:T(8,128)} %fusion.13, f32[32,64,1024]{2,1,0:T(8,128)} %fusion.2, f32[32,64,1024]{2,1,0:T(8,128)} %fusion.16, bf16[32,64,1024]{2,1,0:T(8,128)(2,1)} %get-tuple-element.47, bf16[1024,1024]{1,0:T(8,128)(2,1)} %param.16), kind=kOutput, calls=%fused_computation | convolution fusion | flops 4305453056 | bytes 44040192 | tf_op jit(solution)/shard_map/bte,de->btd/dot_general | solution.py:24
  794.8 5.3 copy.40
  801.5 249.5 %all-reduce.9.cloned.1.call-done = (f32[1024,1024]{0,1:T(8,128)}, f32[1024,1024]{0,1:T(8,128)}, f32[1024,1024]{0,1:T(8,128)}) async-done(((f32[1024,1024]{0,1:T(8,128)}, f32[1024,1024]{0,1:T(8,128)}, f32[1024,1024]{0,1:T(8,128)}), (f32[1024,1024]{0,1:T(8,128)}, f32[1024,1024]{0,1:T(8,128)}, f32[1024,1024]{0,1:T(8,128)})) %all-reduce.9.cloned.1.call-update) | async-done | bytes 12582928 | tf_op jit(solution)/shard_map/psum | solution.py:426
  1051.0 5.3 copy.37
  1056.4 5.3 copy.38
  1061.7 5.4 copy.39
  1068.2 4.8 copy.54
  (87 shorter events, 19.6 us)
Async XLA Ops:
  7.2 733.1 %all-reduce.11.cloned.1.call-start = ((), (), s32[]{:S(2)}) async-start(), calls=%async_computation.2 | async-start | bytes 16777216 | tf_op jit(solution)/shard_map/psum | solution.py:421
  8.8 7.2 copy-start.1
  8.8 7.3 copy-start.19
  21.0 10.4 copy-start.23
  28.4 9.1 copy-start.18
  28.4 9.1 copy-start.21
  28.4 18.5 %collective-permute-start = (bf16[32,3,3072]{2,0,1:T(8,128)(2,1)S(1)}, bf16[32,3,3072]{2,0,1:T(8,128)(2,1)S(1)}, u32[]{:S(2)}, u32[]{:S(2)}) collective-permute-start(bf16[32,3,3072]{2,0,1:T(8,128)(2,1)S(1)} %copy.31), channel_id=1, source_target_pairs={{0,1},{1,2},{2,3},{3,4},{4,5},{5,6},{6,7},{8,9},{9,10},{10,11},{11... | collective-permute-start | bytes 1769480 | tf_op jit(solution)/shard_map/ppermute | solution.py:413
  37.5 6.2 copy-start.15
  37.5 6.8 copy-start.25
  37.5 7.3 copy-start.9
  240.0 10.2 copy-start.2
  240.0 10.2 copy-start.27
  256.3 543.8 %all-reduce.7.cloned.1.call-start = ((), (), s32[]{:S(2)}) async-start(), calls=%async_computation | async-start | bytes 164864 | tf_op jit(solution)/shard_map/psum | solution.py:426
  708.9 10.1 copy-start.7
  709.0 10.9 %copy-start.17 = (f32[8,128]{1,0:T(8,128)S(1)}, f32[8,128]{1,0:T(8,128)}, u32[]{:S(2)}) copy-start(f32[8,128]{1,0:T(8,128)} %get-tuple-element.49) | copy-start | bytes 12292
  709.0 11.4 %copy-start.5 = (bf16[32,64,8]{2,1,0:T(8,128)(2,1)S(1)}, bf16[32,64,8]{2,1,0:T(8,128)(2,1)}, u32[]{:S(2)}) copy-start(bf16[32,64,8]{2,1,0:T(8,128)(2,1)} %get-tuple-element.44) | copy-start | bytes 98308
  723.8 10.2 copy-start.3
  723.8 10.2 copy-start.4
  734.0 6.4 copy-start.10
  740.4 310.7 %all-reduce.9.cloned.1.call-start = ((), (), s32[]{:S(2)}) async-start(), calls=%async_computation.1 | async-start | bytes 25165824 | tf_op jit(solution)/shard_map/psum | solution.py:426
  744.9 9.2 copy-start.20
  744.9 9.2 copy-start.30
  754.1 7.2 copy-start.22
  754.1 7.2 copy-start.29
  (11 other events, 54.2 us)
Sparse Core Ops, SparseCore 0:
  256.5 283.6 all-reduce.10
  740.5 53.2 all-reduce.6
  797.5 253.4 all-reduce.8

commit v2 on v1

--- a/solution.py
+++ b/solution.py
@@ -10,6 +10,10 @@
 CONV_TAPS = 4
 PAD = CONV_TAPS - 1
 SEND_SLOTS = 4
+CHUNK = 64
+LAG_JOIN = 2
+LAG_TOTAL = 5
+LAG_END = 9
 F32 = jnp.float32
 BF16 = jnp.bfloat16
 MESH = pl.DeviceIdType.MESH
@@ -400,6 +404,174 @@
     )(*ins)
 
 
+def tail_kernel(n_seqs, *refs):
+    parts, (h_ref, dg_ref, dq_ref, dk_ref, dv_ref, dl_ref), (wo_ref, wg_ref, wq_ref, wk_ref, wv_ref, wb_ref) = refs[:6], refs[6:12], refs[12:18]
+    sums, (y_ref, dx_ref) = refs[18:24], refs[24:26]
+    own, pair, outer, inner, load_sem, psend, precv, osend, orecv, isend, irecv, store_sem, csend, crecv = refs[26:]
+    step = pl.program_id(0)
+    n_chunks = own.shape[0] // CHUNK
+    last_step = n_chunks + LAG_END
+    me = lax.axis_index('sp')
+    chip = me // 2
+    core = lax.rem(me, 2)
+    partner = me + 1 - 2 * core
+    is_end = (chip == 0) | (chip == 3)
+    is_mid = (chip == 1) | (chip == 2)
+    outer_dev = lax.rem(me + 8 + 2 - 4 * lax.rem(chip, 2), 8)
+    inner_dev = lax.rem(me + 8 - 2 + 4 * lax.rem(chip, 2), 8)
+    group_len = parts[0].shape[0] // 2 // CHUNK
+
+    def rows(idx):
+        return pl.ds(pl.multiple_of(idx * CHUNK, CHUNK), CHUNK)
+
+    def half(idx, which):
+        size = parts[idx].shape[0] // 2
+        return pl.ds(pl.multiple_of(which * size, CHUNK), size)
+
+    def buf_rows(idx):
+        return pl.ds(idx * group_len * CHUNK, parts[idx].shape[0] // 2)
+
+    def remote(src, dst, send_sem, recv_sem, dev):
+        return pltpu.make_async_remote_copy(src_ref=src, dst_ref=dst, send_sem=send_sem, recv_sem=recv_sem, device_id={'sp': dev}, device_id_type=MESH)
+
+    def load_copy(idx):
+        return pltpu.make_async_copy(parts[idx].at[half(idx, core)], own.at[buf_rows(idx)], load_sem.at[idx])
+
+    def pair_copy(idx):
+        return remote(parts[idx].at[half(idx, 1 - core)], pair.at[buf_rows(idx)], psend.at[idx], precv.at[idx], partner)
+
+    def outer_copy(src, idx):
+        return remote(src.at[rows(idx)], outer.at[rows(idx)], osend.at[idx], orecv.at[idx], outer_dev)
+
+    def inner_copy(idx):
+        return remote(own.at[rows(idx)], inner.at[rows(idx)], isend.at[idx], irecv.at[idx], inner_dev)
+
+    def store_copy(src, idx):
+        return pltpu.make_async_copy(src.at[buf_rows(idx)], sums[idx].at[half(idx, core)], store_sem.at[idx])
+
+    def give_copy(src, idx):
+        return remote(src.at[buf_rows(idx)], sums[idx].at[half(idx, core)], csend.at[idx], crecv.at[idx], partner)
+
+    @pl.when(step == 0)
+    def _():
+        barrier = pltpu.get_barrier_semaphore()
+        for other in range(1, 8):
+            pl.semaphore_signal(barrier, inc=1, device_id={'sp': lax.rem(me + other, 8)}, device_id_type=MESH)
+        pl.semaphore_wait(barrier, 7)
+        for idx in range(len(parts)):
+            load_copy(idx).start()
+            pair_copy(idx).start()
+
+    @pl.when(is_end & (step >= 1) & (step <= n_chunks))
+    def _():
+        outer_copy(own, step - 1).start()
+
+    @pl.when(is_mid & (step >= LAG_JOIN + 1) & (step <= n_chunks + LAG_JOIN))
+    def _():
+        inner_copy(step - LAG_JOIN - 1).start()
+
+    @pl.when(is_mid & (step >= LAG_TOTAL + 1) & (step <= n_chunks + LAG_TOTAL))
+    def _():
+        outer_copy(pair, step - LAG_TOTAL - 1).start()
+
+    for idx in range(len(parts)):
+        final = idx * group_len + parts[idx].shape[0] // 2 // CHUNK - 1
+
+        @pl.when(is_mid & (step == final + LAG_TOTAL + 1))
+        def _():
+            store_copy(pair, idx).start()
+            give_copy(pair, idx).start()
+
+        @pl.when(step == idx * group_len)
+        def _():
+            load_copy(idx).wait()
+            pair_copy(idx).wait_recv()
+
+    @pl.when(step < n_seqs)
+    def _():
+        y_ref[0] = lax.dot_general(h_ref[0], wo_ref[...], (((1,), (0,)), ((), ())), preferred_element_type=F32).astype(BF16)
+        total = lax.dot_general(dg_ref[0], wg_ref[...], (((1,), (1,)), ((), ())), preferred_element_type=F32)
+        for grad_ref, w_ref in ((dl_ref, wb_ref), (dq_ref, wq_ref), (dk_ref, wk_ref), (dv_ref, wv_ref)):
+            total = total + lax.dot_general(grad_ref[0], w_ref[...], (((1,), (1,)), ((), ())), preferred_element_type=F32)
+        dx_ref[0] = total.astype(BF16)
+
+    @pl.when(step < n_chunks)
+    def _():
+        own[rows(step)] = own[rows(step)] + pair[rows(step)]
+
+    @pl.when(is_mid & (step >= LAG_JOIN) & (step < n_chunks + LAG_JOIN))
+    def _():
+        idx = step - LAG_JOIN
+        outer_copy(pair, idx).wait_recv()
+        own[rows(idx)] = own[rows(idx)] + outer[rows(idx)]
+
+    @pl.when(is_mid & (step >= LAG_TOTAL) & (step < n_chunks + LAG_TOTAL))
+    def _():
+        idx = step - LAG_TOTAL
+        inner_copy(idx).wait_recv()
+        pair[rows(idx)] = own[rows(idx)] + inner[rows(idx)]
+
+    @pl.when(is_end & (step >= LAG_END) & (step < n_chunks + LAG_END))
+    def _():
+        outer_copy(own, step - LAG_END).wait_recv()
+
+    for idx in range(len(parts)):
+        final = idx * group_len + parts[idx].shape[0] // 2 // CHUNK - 1
+
+        @pl.when(is_end & (step == final + LAG_END))
+        def _():
+            store_copy(outer, idx).start()
+            give_copy(outer, idx).start()
+
+    @pl.when(step == last_step)
+    def _():
+        for idx in range(len(parts)):
+            pair_copy(idx).wait_send()
+            store_copy(outer, idx).wait()
+            give_copy(outer, idx).wait()
+
+        def drain_outer(idx, carry):
+            outer_copy(own, idx).wait_send()
+            return carry
+
+        lax.fori_loop(0, n_chunks, drain_outer, 0)
+
+        @pl.when(is_mid)
+        def _():
+            def drain_inner(idx, carry):
+                inner_copy(idx).wait_send()
+                return carry
+
+            lax.fori_loop(0, n_chunks, drain_inner, 0)
+
+
+def run_tail(parts, acts, weights):
+    n_seqs, seq_dev, model_dim = acts[0].shape
+    n_rows = sum(part.shape[0] for part in parts) // 2
+    n_chunks = n_rows // CHUNK
+    n_parts = len(parts)
+    any_spec = pl.BlockSpec(memory_space=pl.ANY)
+
+    def row_block(arr):
+        return pl.BlockSpec((1,) + tuple(arr.shape[1:]), lambda step: (jnp.minimum(step, n_seqs - 1), 0, 0))
+
+    outs = [jax.ShapeDtypeStruct(part.shape, F32) for part in parts] + [jax.ShapeDtypeStruct(acts[0].shape, BF16)] * 2
+    buf = pltpu.VMEM((n_rows, model_dim), F32)
+    part_sems = pltpu.SemaphoreType.DMA((n_parts,))
+    chunk_sems = pltpu.SemaphoreType.DMA((n_chunks,))
+    return pl.pallas_call(
+        functools.partial(tail_kernel, n_seqs),
+        grid=(n_chunks + LAG_END + 1,),
+        out_shape=outs,
+        in_specs=[any_spec] * n_parts + [row_block(arr) for arr in acts] + [pl.BlockSpec(memory_space=pltpu.VMEM) for _ in weights],
+        out_specs=[any_spec] * n_parts + [row_block(acts[0])] * 2,
+        scratch_shapes=[buf] * 4 + [part_sems] * 3 + [chunk_sems] * 4 + [part_sems] * 3,
+        compiler_params=pltpu.CompilerParams(collective_id=2, has_side_effects=True, vmem_limit_bytes=62 * 1024 * 1024, dimension_semantics=('arbitrary',)),
+        cost_estimate=pl.CostEstimate(flops=250_000_000_000, bytes_accessed=120_000_000, transcendentals=0),
+        name='sum_and_project',
+    )(*parts, *acts, *weights)
+
+
 def solution(mesh):
     groups = mesh.shape['sp']
     to_next = [(source, source + 1) for source in range(groups - 1)]
@@ -417,15 +589,20 @@
         d_hidden = back_project(dy_out, w_out).astype(BF16)
         norm_f = norm_weight.astype(F32).reshape(1, HEAD_DIM)
         hidden, d_gate, d_attn, q_act, k_act, t_mat, s_mat, r_mat, d_mat, dnorm = run_forward(groups, projs, tails, taps, logits, gate_pre, d_hidden, norm_f)
-        y_out = project(hidden, w_out).astype(BF16)
-        early = lax.psum((weight_grad(x_in, d_gate), weight_grad(hidden, dy_out)), 'sp')
         dp_q, dp_k, dp_v, d_logit, dtaps = run_backward(groups, projs, tails, taps, logits, d_attn, q_act, k_act, t_mat, s_mat, r_mat, d_mat)
-        dtaps = jnp.sum(dtaps, axis=2)
-        late_parts = (weight_grad(x_in, dp_q), weight_grad(x_in, dp_k), weight_grad(x_in, dp_v), weight_grad(x_in, d_logit), dtaps, jnp.sum(dnorm, axis=0))
-        late_parts, early = lax.optimization_barrier((late_parts, early))
-        late = lax.psum(late_parts, 'sp')
-        dx_acc = back_project(d_gate, w_gate) + back_project(d_logit, w_beta) + back_project(dp_q, w_query) + back_project(dp_k, w_key) + back_project(dp_v, w_value)
-        return (y_out, dx_acc.astype(BF16), late[0], late[1], late[2], late[3], late[4][0], late[4][1], late[4][2], early[0], late[5], early[1])
+        model_dim = x_in.shape[2]
+        small = jnp.concatenate([
+            jnp.einsum('bte,btd->ed', d_logit, x_in, preferred_element_type=F32),
+            jnp.sum(dtaps, axis=2).reshape(3 * CONV_TAPS, model_dim),
+            jnp.pad(jnp.sum(dnorm, axis=0, keepdims=True), ((0, 0), (0, model_dim - HEAD_DIM)))])
+        n_heads = w_beta.shape[1]
+        small = jnp.pad(small, ((0, 2 * CHUNK - small.shape[0]), (0, 0)))
+        grads = (weight_grad(x_in, d_gate), weight_grad(hidden, dy_out), weight_grad(x_in, dp_q), weight_grad(x_in, dp_k), weight_grad(x_in, dp_v), small)
+        dw_gate, dw_out, dw_q, dw_k, dw_v, small, y_out, dx_in = run_tail(
+            grads, (hidden, d_gate, dp_q, dp_k, dp_v, d_logit), (w_out, w_gate, w_query, w_key, w_value, w_beta))
+        dtaps = small[n_heads:n_heads + 3 * CONV_TAPS].reshape(3, CONV_TAPS, model_dim)
+        dnorm = small[n_heads + 3 * CONV_TAPS, :HEAD_DIM]
+        return (y_out, dx_in, dw_q, dw_k, dw_v, small[:n_heads].T, dtaps[0], dtaps[1], dtaps[2], dw_gate, dnorm, dw_out)
 
     in_specs = (seq_spec, seq_spec) + (full_mat,) * 8 + (P(None), full_mat)
     out_specs = (seq_spec, seq_spec) + (part_mat,) * 8 + (P('dp'), part_mat)

time: 1090 us -> 883 us (0.81)
  waiting for transfers between devices: 250 us -> 0.01 us
  Pallas kernels: 644 us -> 762 us
  matrix products: 131 us -> 71.7 us
  between operations: 14.5 us -> 1.37 us
    pallas_call x0 -> x1, Pallas kernels: none -> 272 us  [run_tail(): pl.pallas_call(functools.partial(tail_kernel, n_seqs), grid=(n_chunks + L...]
    psum x3 -> x0, waiting for transfers between devices: 250 us -> none  [the longest x2 250 us: local_step(): late = lax.psum(late_parts, 'sp')]
    pallas_call x1, Pallas kernels: 453 us -> 299 us  [run_backward(): pl.pallas_call(functools.partial(backward_kernel, groups), grid=(n_seqs,)...]
    dot_general x6 -> x1, matrix products: 54.4 us -> 6.26 us  [back_project(): jnp.einsum('bte,de->btd', grad_in, weight, preferred_element_type=F32)]
    dot_general x6 -> x5, matrix products: 46.3 us -> 35.1 us  [weight_grad(): jnp.einsum('btd,bte->de', act_in, grad_in, preferred_element_type=F32)]
    dot_general x6 -> x5, matrix products: 30.7 us -> 27.3 us  [project(): return jnp.einsum('btd,de->bte', act_in, weight, preferred_element_type=F32)]
    unnamed x69 -> x62, local copies, waits for them, and re-layouts: 30.8 us -> 28.4 us
  transfers between devices with their start and end apart: 4 -> 1, of which waited for: 1 -> 0; matrix products, arithmetic and copies ran while one was open for 10% -> 2% of each run, Pallas kernels for 42% -> 0%
where the time goes in v2:
time: 883 us; the launch traced here: 876 us
  Pallas kernels  762 us (86%)
  matrix products  71.7 us (8%)
  local copies, waits for them, and re-layouts  35.3 us (4%)
    pallas_call x1, Pallas kernels, run_backward(): pl.pallas_call(functools.partial(backward_kernel, groups), grid=(n_seqs,)...  299 us
    pallas_call x1, Pallas kernels, run_tail(): pl.pallas_call(functools.partial(tail_kernel, n_seqs), grid=(n_chunks + L...  272 us
    pallas_call x1, Pallas kernels, run_forward(): pl.pallas_call(functools.partial(forward_kernel, groups), grid=(n_seqs,),...  191 us
    dot_general x5, matrix products, weight_grad(): jnp.einsum('btd,bte->de', act_in, grad_in, preferred_element_type=F32)  35.1 us
    unnamed x62, local copies, waits for them, and re-layouts  28.4 us
    dot_general x5, matrix products, project(): return jnp.einsum('btd,de->bte', act_in, weight, preferred_element_type=F32)  27.3 us
  transfers between devices with their start and end apart: 1, of which 0 were waited for; matrix products, arithmetic and copies ran while one was open for 2% of the time, Pallas kernels for 0%

profile of v2, /device:TPU:0, one launch (start us, length us, event | category | flops | bytes accessed | tf_op | source)
XLA Modules:
  0.0 876.2 jit_solution(10836483446035988780)
XLA Ops:
  0.7 7.5 convolution_convert_fusion.4.pq_ref
  8.4 1.9 copy-done.9
  10.2 4.7 convolution_convert_fusion.3.pk_ref
  15.1 4.8 convolution_convert_fusion.2.pv_ref
  20.7 3.0 collective-permute-start
  23.7 6.1 convolution_convert_fusion.1.z_ref
  29.9 6.3 convolution_convert_fusion.dh_ref
  38.2 4.2 convolution_convert_fusion.5.logit_ref
  43.8 191.1 %delta_forward.1 = (bf16[32,64,1024]{2,1,0:T(8,128)(2,1)}, bf16[32,64,1024]{2,1,0:T(8,128)(2,1)}, bf16[32,8,64,128]{3,2,1,0:T(8,128)(2,1)}, bf16[32,8,64,128]{3,...) custom-call(bf16[32,64,1024]{2,1,0:T(8,128)(2,1)} %copy-done.9, ...), custom_call_target="tpu_custom_call" | custom-call | flops 199999995904 | bytes 120000000 | tf_op jit(solution)/shard_map/delta_forward/pallas_call | solution.py:355
  234.8 299.1 %delta_backward.1 = (bf16[32,64,1024]{2,1,0:T(8,128)(2,1)}, bf16[32,64,1024]{2,1,0:T(8,128)(2,1)}, bf16[32,64,1024]{2,1,0:T(8,128)(2,1)}, bf16[32,64,8]{2,1,0:T(8,128)(2,1)}, f32[3,4,8,1024]{3,2,1,0:T(8,128)}) custom-call(bf16[32,64,1024]{2,1,0:T(8,128)(2,1)} %copy-done.9, bf16[32,64,1024]{2,1,0:T(8,128)(2,1)} %copy-done.10, ...), custom_call_target="tpu_custom_call" | custom-call | flops 249999998976 | bytes 120000000 | tf_op jit(solution)/shard_map/delta_backward/pallas_call | solution.py:382
  535.1 3.0 convolution_bitcast_fusion.5
  539.0 10.2 %convolution_bitcast_fusion.refs_4_ = f32[1024,1024]{1,0:T(8,128)} fusion(bf16[32,64,1024]{2,1,0:T(8,128)(2,1)} %get-tuple-element.46.refs_10_, bf16[32,64,1024]{2,1,0:T(8,128)(2,1)} %param.12), kind=kOutput, calls=%fused_computation.5 | convolution fusion | flops 4294967296 | bytes 12582912 | tf_op jit(solution)/shard_map/btd,bte->de/dot_general | solution.py:32
  549.2 6.2 convolution_bitcast_fusion.1.refs_3_
  555.4 6.2 convolution_bitcast_fusion.2.refs_2_
  561.6 6.1 convolution_bitcast_fusion.3.refs_1_
  567.7 6.4 convolution_bitcast_fusion.4.refs_0_
  574.1 272.0 %sum_and_project.1 = (f32[1024,1024]{1,0:T(8,128)}, f32[1024,1024]{1,0:T(8,128)}, f32[1024,1024]{1,0:T(8,128)}, f32[1024,1024]{1,0:T(8,128)}, f32[1024,1024]{1,0...) custom-call(f32[1024,1024]{1,0:T(8,128)} %convolution_bitcast_fusion.4.refs_0_, ...), custom_call_target="tpu_custom_call" | custom-call | flops 249999998976 | bytes 120000000 | tf_op jit(solution)/shard_map/sum_and_project/pallas_call | solution.py:562
  850.2 5.1 copy.58
  855.2 2.1 copy.59
  858.9 2.1 copy.60
  862.7 2.1 copy.61
  866.4 2.1 copy.62
  870.1 2.1 copy.63
  873.8 2.0 copy.64
  (71 shorter events, 18.3 us)
Async XLA Ops:
  0.6 9.6 %copy-start = (bf16[32,64,1024]{2,1,0:T(8,128)(2,1)S(1)}, bf16[32,64,1024]{2,1,0:T(8,128)(2,1)}, u32[]{:S(2)}) copy-start(bf16[32,64,1024]{2,1,0:T(8,128)(2,1)} %param.12) | copy-start | bytes 12582916
  0.7 9.6 %copy-start.18 = (bf16[1024,1024]{1,0:T(8,128)(2,1)S(1)}, bf16[1024,1024]{1,0:T(8,128)(2,1)}, u32[]{:S(2)}) copy-start(bf16[1024,1024]{1,0:T(8,128)(2,1)} %refs_15_.1) | copy-start | bytes 6291460
  10.2 4.9 copy-start.19
  14.9 5.0 copy-start.10
  15.1 8.6 copy-start.20
  19.9 9.9 %copy-start.11 = (bf16[32,64,1024]{2,1,0:T(8,128)(2,1)}, bf16[32,64,1024]{2,1,0:T(8,128)(2,1)S(1)}, u32[]{:S(2)}) copy-start(bf16[32,64,1024]{2,1,0:T(8,128)(2,1)S(1)} %convolution_convert_fusion.2.pv_ref) | copy-start | bytes 12582916
  20.7 9.2 %copy-start.16 = (bf16[32,64,1024]{2,1,0:T(8,128)(2,1)S(1)}, bf16[32,64,1024]{2,1,0:T(8,128)(2,1)}, u32[]{:S(2)}) copy-start(bf16[32,64,1024]{2,1,0:T(8,128)(2,1)} %param.13) | copy-start | bytes 12582916
  20.7 9.2 %copy-start.21 = (bf16[1024,1024]{1,0:T(8,128)(2,1)S(1)}, bf16[1024,1024]{1,0:T(8,128)(2,1)}, u32[]{:S(2)}) copy-start(bf16[1024,1024]{1,0:T(8,128)(2,1)} %refs_12_.1) | copy-start | bytes 6291460
  20.7 21.7 %collective-permute-start = (bf16[32,3,3072]{2,0,1:T(8,128)(2,1)S(1)}, bf16[32,3,3072]{2,0,1:T(8,128)(2,1)S(1)}, u32[]{:S(2)}, u32[]{:S(2)}) collective-permute-start(bf16[32,3,3072]{2,0,1:T(8,128)(2,1)S(1)} %copy.31), channel_id=1, source_target_pairs={{0,1},{1,2},{2,3},{3,4},{4,5},{5,6},{6,7},{8,9},{9,10},{10,11},{11... | collective-permute-start | bytes 1769480 | tf_op jit(solution)/shard_map/ppermute | solution.py:585
  29.8 6.3 copy-start.12
  29.8 6.3 copy-start.13
  29.9 6.3 copy-start.14
  29.9 6.9 copy-start.8
  29.9 7.8 copy-start.22
  533.9 4.2 copy-start.15
  539.0 10.2 %copy-start.1 = (bf16[32,64,1024]{2,1,0:T(8,128)(2,1)S(1)}, bf16[32,64,1024]{2,1,0:T(8,128)(2,1)}, u32[]{:S(2)}) copy-start(bf16[32,64,1024]{2,1,0:T(8,128)(2,1)} %param.12) | copy-start | bytes 12582916
  539.0 10.2 %copy-start.26 = (bf16[32,64,1024]{2,1,0:T(8,128)(2,1)S(1)}, bf16[32,64,1024]{2,1,0:T(8,128)(2,1)}, u32[]{:S(2)}) copy-start(bf16[32,64,1024]{2,1,0:T(8,128)(2,1)} %get-tuple-element.45.refs_9_) | copy-start | bytes 12582916
  549.2 6.2 copy-start.25
  555.4 6.2 copy-start.17
  555.4 6.2 copy-start.23
  561.6 6.1 copy-start.24
  850.2 5.1 copy-start.7
  855.2 3.7 copy-start.6
  858.9 3.7 copy-start.5
  (4 other events, 13.1 us)

commit v3 on v2

--- a/solution.py
+++ b/solution.py
@@ -41,7 +41,21 @@
     return high, (value - high.astype(F32)).astype(BF16)
 
 
+def rows_cat(*parts):
+    return jnp.concatenate(parts, axis=1)
+
+
+def twice(value, axis):
+    return jnp.concatenate([value, value], axis=axis)
+
+
+def joined(pair, axis):
+    return jnp.concatenate(pair, axis=axis)
+
+
 def dot_er(lhs, rhs, lhs_dim, rhs_dim):
+    if lhs_dim == 2 and lhs.shape[2] == HEAD_DIM:
+        return bdot(twice(lhs, 2), joined(rhs, rhs_dim), 2, rhs_dim)
     return bdot(lhs, rhs[0], lhs_dim, rhs_dim) + bdot(lhs, rhs[1], lhs_dim, rhs_dim)
 
 
@@ -50,6 +64,14 @@
 
 
 def dot_rr(lhs, rhs, lhs_dim, rhs_dim):
+    if lhs_dim == 2:
+        n_rows = lhs[0].shape[1]
+        both = rows_cat(*lhs)
+        if both.shape[2] == HEAD_DIM:
+            prod = bdot(twice(both, 2), joined(rhs, rhs_dim), 2, rhs_dim)
+            return prod[:, :n_rows] + prod[:, n_rows:]
+        prod = bdot(both, rhs[0], 2, rhs_dim)
+        return prod[:, :n_rows] + (prod[:, n_rows:] + bdot(lhs[0], rhs[1], 2, rhs_dim))
     return bdot(lhs[0], rhs[0], lhs_dim, rhs_dim) + (bdot(lhs[0], rhs[1], lhs_dim, rhs_dim) + bdot(lhs[1], rhs[0], lhs_dim, rhs_dim))
 
 
@@ -102,7 +124,7 @@
 
 def forward_kernel(groups, pq_ref, pk_ref, pv_ref, tail_ref, taps_ref, logit_ref, z_ref, dh_ref, norm_ref,
                    h_ref, dz_ref, do_ref, q_ref, k_ref, t_ref, s_ref, r_ref, d_ref, dnorm_ref,
-                   recv, send, ext, v_buf, o_buf, send_sem, recv_sem):
+                   recv, send, ext, v_buf, o_buf, score_buf, send_sem, recv_sem):
     step = pl.program_id(0)
     n_steps = pl.num_programs(0)
     me = lax.axis_index('sp')
@@ -120,6 +142,10 @@
     def _():
         entry_barrier(me, groups)
         dnorm_ref[...] = jnp.zeros_like(dnorm_ref)
+
+        @pl.when(me == 0)
+        def _():
+            recv[0] = jnp.zeros(recv.shape[1:], F32)
 
     def act_head(head, carry):
         cols = head_cols(head)
@@ -141,32 +167,30 @@
     k_all = k_ref[0]
     row_idx = lax.broadcasted_iota(jnp.int32, (1, seq_dev, seq_dev), 1)
     col_idx = lax.broadcasted_iota(jnp.int32, (1, seq_dev, seq_dev), 2)
-    gram = bdot(k_all, k_all, 2, 2)
+    kq_all = rows_cat(k_all, q_all)
+    kq_prod = bdot(kq_all, k_all, 2, 2)
+    gram = kq_prod[:, :seq_dev]
+    score_buf[...] = jnp.where(row_idx >= col_idx, kq_prod[:, seq_dev:], 0.0)
     t_ref[0] = block_inverse(jnp.where(row_idx > col_idx, beta3 * gram, 0.0), row_idx, col_idx)
 
     @pl.when(me > 0)
     def _():
         hop(slot, step).wait_recv()
 
-    @pl.when(me == 0)
-    def _():
-        recv[step] = jnp.zeros(recv.shape[1:], F32)
-
     @pl.when((me < groups - 1) & (step >= SEND_SLOTS))
     def _():
         hop(slot, step).wait_send()
 
-    state = recv[step]
+    state = recv[step * jnp.minimum(me, 1)]
     s_ref[0] = state
-    state_split = split(state)
-    resid = v_buf[...].astype(F32) - dot_er(k_all, state_split, 2, 1)
+    kq_state = dot_er(rows_cat(k_ref[0], q_ref[0]), split(state), 2, 1)
+    resid = v_buf[...].astype(F32) - kq_state[:, :seq_dev]
     r_ref[0] = resid
     delta = dot_rr(split(t_ref[0]), split(beta3 * resid), 2, 1)
     d_ref[0] = delta
     delta_split = split(delta)
-    send[slot] = state + dot_er(k_all, delta_split, 1, 1)
-    scores = jnp.where(row_idx >= col_idx, bdot(q_all, k_all, 2, 2), 0.0)
-    o_buf[...] = (dot_er(q_all, state_split, 2, 1) + dot_rr(split(scores), delta_split, 2, 1)).astype(BF16).astype(F32)
+    send[slot] = state + dot_er(k_ref[0], delta_split, 1, 1)
+    o_buf[...] = (kq_state[:, seq_dev:] + dot_rr(split(score_buf[...]), delta_split, 2, 1)).astype(BF16).astype(F32)
 
     @pl.when(me < groups - 1)
     def _():
@@ -202,7 +226,7 @@
 
 def backward_kernel(groups, pq_ref, pk_ref, pv_ref, tail_ref, taps_ref, logit_ref, do_ref, q_ref, k_ref, t_ref, s_ref, r_ref, d_ref,
                     dpq_ref, dpk_ref, dpv_ref, dlogit_ref, dtaps_ref,
-                    recv, send, front, front_send, ext, dext, dact, send_sem, recv_sem, fsend_sem, frecv_sem):
+                    recv, send, front, front_send, ext, dext, dact, gram_buf, delta_buf, state_buf, rhs_buf, send_sem, recv_sem, fsend_sem, frecv_sem):
     step = pl.program_id(0)
     n_steps = pl.num_programs(0)
     me = lax.axis_index('sp')
@@ -227,60 +251,64 @@
         entry_barrier(me, groups)
         dtaps_ref[...] = jnp.zeros_like(dtaps_ref)
 
+        @pl.when(me == groups - 1)
+        def _():
+            recv[0] = jnp.zeros(recv.shape[1:], F32)
+            front[0] = jnp.zeros(front.shape[1:], F32)
+
     sig_beta = jax.nn.sigmoid(logit_ref[0].astype(F32))
     beta3 = head_columns(sig_beta.astype(BF16).astype(F32), n_heads)
-    q_all = q_ref[0]
-    k_all = k_ref[0]
-    d_out = do_ref[0]
+    from_next = step * jnp.minimum(groups - 1 - me, 1)
     row_idx = lax.broadcasted_iota(jnp.int32, (1, seq_dev, seq_dev), 1)
     col_idx = lax.broadcasted_iota(jnp.int32, (1, seq_dev, seq_dev), 2)
-    gram = bdot(k_all, k_all, 2, 2)
-    scores = jnp.where(row_idx >= col_idx, bdot(q_all, k_all, 2, 2), 0.0)
-    t_split = split(t_ref[0])
-    delta_split = split(d_ref[0])
-    state_split = split(s_ref[0])
-    d_delta_own = dot_re(split(scores), d_out, 1, 1)
-    state_own = bdot(q_all, d_out, 1, 1)
-    d_scores = jnp.where(row_idx >= col_idx, dot_er(d_out, delta_split, 2, 2), 0.0).astype(BF16)
-    dact[0] = (dot_er(d_out, state_split, 2, 2) + bdot(d_scores, k_all, 2, 1)).astype(BF16)
+    kq_prod = bdot(rows_cat(k_ref[0], q_ref[0]), k_ref[0], 2, 2)
+    gram_buf[...] = kq_prod[:, :seq_dev]
+    scores = jnp.where(row_idx >= col_idx, kq_prod[:, seq_dev:], 0.0)
+    delta_buf[...] = dot_re(split(scores), do_ref[0], 1, 1)
+    state_buf[...] = bdot(q_ref[0], do_ref[0], 1, 1)
 
     @pl.when(me < groups - 1)
     def _():
         hop(slot, step).wait_recv()
-
-    @pl.when(me == groups - 1)
-    def _():
-        recv[step] = jnp.zeros(recv.shape[1:], F32)
-        front[step] = jnp.zeros(front.shape[1:], F32)
 
     @pl.when((me > 0) & (step >= SEND_SLOTS))
     def _():
         hop(slot, step).wait_send()
         front_hop(slot, step).wait_send()
 
-    d_state = recv[step]
-    d_state_split = split(d_state)
-    d_delta = d_delta_own + dot_er(k_all, d_state_split, 2, 1)
-    d_rhs = dot_rr(t_split, split(d_delta), 1, 1)
+    d_state = recv[from_next]
+    d_delta = delta_buf[...] + dot_er(k_ref[0], split(d_state), 2, 1)
+    d_rhs = dot_rr(split(t_ref[0]), split(d_delta), 1, 1)
     d_resid = beta3 * d_rhs
-    d_resid_split = split(d_resid)
-    send[slot] = d_state + state_own - dot_er(k_all, d_resid_split, 1, 1)
+    rhs_buf[...] = d_rhs
+    send[slot] = d_state + state_buf[...] - dot_er(k_ref[0], split(d_resid), 1, 1)
     dact[2] = d_resid.astype(BF16)
-    d_low = jnp.where(row_idx > col_idx, -dot_rr(split(d_rhs), delta_split, 2, 2), 0.0)
-    d_beta = jnp.sum(d_rhs * r_ref[0], axis=-1, keepdims=True) + jnp.sum(d_low * gram, axis=-1, keepdims=True)
+
+    d_out = do_ref[0]
+    delta_split = split(d_ref[0])
+    d_rhs = rhs_buf[...]
+    by_delta = bdot(twice(rows_cat(d_out, *split(d_rhs)), 2), joined(delta_split, 2), 2, 2)
+
+    @pl.when(me > 0)
+    def _():
+        hop(slot, step).start()
+
+    d_scores = jnp.where(row_idx >= col_idx, by_delta[:, :seq_dev], 0.0).astype(BF16)
+    d_low = jnp.where(row_idx > col_idx, -(by_delta[:, seq_dev:2 * seq_dev] + by_delta[:, 2 * seq_dev:]), 0.0)
+    d_beta = jnp.sum(d_rhs * r_ref[0], axis=-1, keepdims=True) + jnp.sum(d_low * gram_buf[...], axis=-1, keepdims=True)
     d_gram = (beta3 * d_low).astype(BF16)
-    d_key = dot_rr(delta_split, d_state_split, 2, 2) - dot_rr(d_resid_split, state_split, 2, 2)
-    d_key = d_key + bdot(d_gram, k_all, 2, 1) + bdot(d_gram, k_all, 1, 1) + bdot(d_scores, q_all, 1, 1)
+    by_state = bdot(twice(rows_cat(d_out, *split(beta3 * d_rhs)), 2), joined(split(s_ref[0]), 2), 2, 2)
+    k_all = k_ref[0]
+    by_key = bdot(rows_cat(d_scores, d_gram), k_all, 2, 1)
+    dact[0] = (by_state[:, :seq_dev] + by_key[:, :seq_dev]).astype(BF16)
+    d_key = by_key[:, seq_dev:] + bdot(rows_cat(d_gram, d_scores), rows_cat(k_all, q_ref[0]), 1, 1)
+    d_key = d_key + dot_rr(delta_split, split(recv[from_next]), 2, 2) - (by_state[:, seq_dev:2 * seq_dev] + by_state[:, 2 * seq_dev:])
     dact[1] = d_key.astype(BF16)
     lane_idx = lax.broadcasted_iota(jnp.int32, (seq_dev, n_heads), 1)
     beta_grad = jnp.zeros((seq_dev, n_heads), F32)
     for head in range(n_heads):
         beta_grad = beta_grad + jnp.where(lane_idx == head, d_beta[head], 0.0)
     dlogit_ref[0] = (beta_grad.astype(BF16).astype(F32) * sig_beta * (1.0 - sig_beta)).astype(BF16)
-
-    @pl.when(me > 0)
-    def _():
-        hop(slot, step).start()
 
     def act_head(head, carry):
         cols = head_cols(head)
@@ -316,7 +344,7 @@
         cols = head_cols(head)
         for branch in range(3):
             taps = taps_ref[branch, :, cols]
-            dext[branch, pl.ds(seq_dev, 8), cols] = front[step, branch, :, cols]
+            dext[branch, pl.ds(seq_dev, 8), cols] = front[from_next, branch, :, cols]
             total = dext[branch, pl.ds(PAD, seq_dev), cols] * taps[0:1]
             for tap_idx in range(1, CONV_TAPS):
                 total = total + dext[branch, pl.ds(PAD - tap_idx, seq_dev), cols] * taps[tap_idx:tap_idx + 1]
@@ -364,6 +392,7 @@
             pltpu.VMEM((3, seq_dev + 8, model_dim), F32),
             pltpu.VMEM((n_heads, seq_dev, HEAD_DIM), BF16),
             pltpu.VMEM((n_heads, seq_dev, HEAD_DIM), F32),
+            pltpu.VMEM((n_heads, seq_dev, seq_dev), F32),
             pltpu.SemaphoreType.DMA((SEND_SLOTS,)),
             pltpu.SemaphoreType.DMA((n_seqs,)),
         ],
@@ -393,6 +422,10 @@
             pltpu.VMEM((3, seq_dev + 8, model_dim), F32),
             pltpu.VMEM((3, seq_dev + 8, model_dim), F32),
             pltpu.VMEM((3, n_heads, seq_dev, HEAD_DIM), BF16),
+            pltpu.VMEM((n_heads, seq_dev, seq_dev), F32),
+            pltpu.VMEM((n_heads, seq_dev, HEAD_DIM), F32),
+            pltpu.VMEM((n_heads, HEAD_DIM, HEAD_DIM), F32),
+            pltpu.VMEM((n_heads, seq_dev, HEAD_DIM), F32),
             pltpu.SemaphoreType.DMA((SEND_SLOTS,)),
             pltpu.SemaphoreType.DMA((n_seqs,)),
             pltpu.SemaphoreType.DMA((SEND_SLOTS,)),

time: 883 us -> 865 us (0.980)
  Pallas kernels: 762 us -> 744 us
    pallas_call x1, Pallas kernels: 191 us -> 180 us  [run_forward(): pl.pallas_call(functools.partial(forward_kernel, groups), grid=(n_seqs,),...]
where the time goes in v3:
time: 865 us; the launch traced here: 858 us
  Pallas kernels  744 us (86%)
  matrix products  71.7 us (8%)
  local copies, waits for them, and re-layouts  35.3 us (4%)
    pallas_call x1, Pallas kernels, run_backward(): pl.pallas_call(functools.partial(backward_kernel, groups), grid=(n_seqs,)...  292 us
    pallas_call x1, Pallas kernels, run_tail(): pl.pallas_call(functools.partial(tail_kernel, n_seqs), grid=(n_chunks + L...  272 us
    pallas_call x1, Pallas kernels, run_forward(): pl.pallas_call(functools.partial(forward_kernel, groups), grid=(n_seqs,),...  180 us
    dot_general x5, matrix products, weight_grad(): jnp.einsum('btd,bte->de', act_in, grad_in, preferred_element_type=F32)  35.1 us
    unnamed x62, local copies, waits for them, and re-layouts  28.4 us
    dot_general x5, matrix products, project(): return jnp.einsum('btd,de->bte', act_in, weight, preferred_element_type=F32)  27.3 us
  transfers between devices with their start and end apart: 1, of which 0 were waited for; matrix products, arithmetic and copies ran while one was open for 2% of the time, Pallas kernels for 0%

profile of v3, /device:TPU:0, one launch (start us, length us, event | category | flops | bytes accessed | tf_op | source)
XLA Modules:
  0.0 858.0 jit_solution(17707585449716774458)
XLA Ops:
  0.7 7.5 convolution_convert_fusion.4.pq_ref
  8.4 1.9 copy-done.9
  10.2 4.7 convolution_convert_fusion.3.pk_ref
  15.1 4.8 convolution_convert_fusion.2.pv_ref
  20.7 3.0 collective-permute-start
  23.7 6.1 convolution_convert_fusion.1.z_ref
  29.9 6.3 convolution_convert_fusion.dh_ref
  38.2 4.2 convolution_convert_fusion.5.logit_ref
  43.8 180.0 %delta_forward.1 = (bf16[32,64,1024]{2,1,0:T(8,128)(2,1)}, bf16[32,64,1024]{2,1,0:T(8,128)(2,1)}, bf16[32,8,64,128]{3,2,1,0:T(8,128)(2,1)}, bf16[32,8,64,128]{3,...) custom-call(bf16[32,64,1024]{2,1,0:T(8,128)(2,1)} %copy-done.9, ...), custom_call_target="tpu_custom_call" | custom-call | flops 199999995904 | bytes 120000000 | tf_op jit(solution)/shard_map/delta_forward/pallas_call | solution.py:383
  223.8 291.9 %delta_backward.1 = (bf16[32,64,1024]{2,1,0:T(8,128)(2,1)}, bf16[32,64,1024]{2,1,0:T(8,128)(2,1)}, bf16[32,64,1024]{2,1,0:T(8,128)(2,1)}, bf16[32,64,8]{2,1,0:T(8,128)(2,1)}, f32[3,4,8,1024]{3,2,1,0:T(8,128)}) custom-call(bf16[32,64,1024]{2,1,0:T(8,128)(2,1)} %copy-done.9, bf16[32,64,1024]{2,1,0:T(8,128)(2,1)} %copy-done.10, ...), custom_call_target="tpu_custom_call" | custom-call | flops 249999998976 | bytes 120000000 | tf_op jit(solution)/shard_map/delta_backward/pallas_call | solution.py:411
  516.9 3.0 convolution_bitcast_fusion.5
  520.8 10.2 %convolution_bitcast_fusion.refs_4_ = f32[1024,1024]{1,0:T(8,128)} fusion(bf16[32,64,1024]{2,1,0:T(8,128)(2,1)} %get-tuple-element.46.refs_10_, bf16[32,64,1024]{2,1,0:T(8,128)(2,1)} %param.12), kind=kOutput, calls=%fused_computation.5 | convolution fusion | flops 4294967296 | bytes 12582912 | tf_op jit(solution)/shard_map/btd,bte->de/dot_general | solution.py:32
  531.0 6.2 convolution_bitcast_fusion.1.refs_3_
  537.2 6.2 convolution_bitcast_fusion.2.refs_2_
  543.4 6.1 convolution_bitcast_fusion.3.refs_1_
  549.5 6.4 convolution_bitcast_fusion.4.refs_0_
  555.9 272.0 %sum_and_project.1 = (f32[1024,1024]{1,0:T(8,128)}, f32[1024,1024]{1,0:T(8,128)}, f32[1024,1024]{1,0:T(8,128)}, f32[1024,1024]{1,0:T(8,128)}, f32[1024,1024]{1,0...) custom-call(f32[1024,1024]{1,0:T(8,128)} %convolution_bitcast_fusion.4.refs_0_, ...), custom_call_target="tpu_custom_call" | custom-call | flops 249999998976 | bytes 120000000 | tf_op jit(solution)/shard_map/sum_and_project/pallas_call | solution.py:595
  832.0 5.1 copy.58
  837.0 2.1 copy.59
  840.7 2.1 copy.60
  844.4 2.1 copy.61
  848.1 2.1 copy.62
  851.8 2.1 copy.63
  855.5 2.0 copy.64
  (71 shorter events, 18.3 us)
Async XLA Ops:
  0.6 9.6 %copy-start = (bf16[32,64,1024]{2,1,0:T(8,128)(2,1)S(1)}, bf16[32,64,1024]{2,1,0:T(8,128)(2,1)}, u32[]{:S(2)}) copy-start(bf16[32,64,1024]{2,1,0:T(8,128)(2,1)} %param.12) | copy-start | bytes 12582916
  0.7 9.6 %copy-start.18 = (bf16[1024,1024]{1,0:T(8,128)(2,1)S(1)}, bf16[1024,1024]{1,0:T(8,128)(2,1)}, u32[]{:S(2)}) copy-start(bf16[1024,1024]{1,0:T(8,128)(2,1)} %refs_15_.1) | copy-start | bytes 6291460
  10.2 4.9 copy-start.19
  14.9 5.0 copy-start.10
  15.1 8.6 %copy-start.20 = (bf16[1024,1024]{1,0:T(8,128)(2,1)S(1)}, bf16[1024,1024]{1,0:T(8,128)(2,1)}, u32[]{:S(2)}) copy-start(bf16[1024,1024]{1,0:T(8,128)(2,1)} %refs_13_.1) | copy-start | bytes 6291460
  19.9 9.9 %copy-start.11 = (bf16[32,64,1024]{2,1,0:T(8,128)(2,1)}, bf16[32,64,1024]{2,1,0:T(8,128)(2,1)S(1)}, u32[]{:S(2)}) copy-start(bf16[32,64,1024]{2,1,0:T(8,128)(2,1)S(1)} %convolution_convert_fusion.2.pv_ref) | copy-start | bytes 12582916
  20.7 9.2 %copy-start.16 = (bf16[32,64,1024]{2,1,0:T(8,128)(2,1)S(1)}, bf16[32,64,1024]{2,1,0:T(8,128)(2,1)}, u32[]{:S(2)}) copy-start(bf16[32,64,1024]{2,1,0:T(8,128)(2,1)} %param.13) | copy-start | bytes 12582916
  20.7 9.2 %copy-start.21 = (bf16[1024,1024]{1,0:T(8,128)(2,1)S(1)}, bf16[1024,1024]{1,0:T(8,128)(2,1)}, u32[]{:S(2)}) copy-start(bf16[1024,1024]{1,0:T(8,128)(2,1)} %refs_12_.1) | copy-start | bytes 6291460
  20.7 21.7 %collective-permute-start = (bf16[32,3,3072]{2,0,1:T(8,128)(2,1)S(1)}, bf16[32,3,3072]{2,0,1:T(8,128)(2,1)S(1)}, u32[]{:S(2)}, u32[]{:S(2)}) collective-permute-start(bf16[32,3,3072]{2,0,1:T(8,128)(2,1)S(1)} %copy.31), channel_id=1, source_target_pairs={{0,1},{1,2},{2,3},{3,4},{4,5},{5,6},{6,7},{8,9},{9,10},{10,11},{11... | collective-permute-start | bytes 1769480 | tf_op jit(solution)/shard_map/ppermute | solution.py:618
  29.8 6.3 copy-start.12
  29.8 6.3 copy-start.13
  29.9 6.3 copy-start.14
  29.9 6.9 copy-start.8
  29.9 7.8 copy-start.22
  515.7 4.2 copy-start.15
  520.8 10.2 %copy-start.1 = (bf16[32,64,1024]{2,1,0:T(8,128)(2,1)S(1)}, bf16[32,64,1024]{2,1,0:T(8,128)(2,1)}, u32[]{:S(2)}) copy-start(bf16[32,64,1024]{2,1,0:T(8,128)(2,1)} %param.12) | copy-start | bytes 12582916
  520.8 10.2 %copy-start.26 = (bf16[32,64,1024]{2,1,0:T(8,128)(2,1)S(1)}, bf16[32,64,1024]{2,1,0:T(8,128)(2,1)}, u32[]{:S(2)}) copy-start(bf16[32,64,1024]{2,1,0:T(8,128)(2,1)} %get-tuple-element.45.refs_9_) | copy-start | bytes 12582916
  531.0 6.2 copy-start.25
  537.2 6.2 copy-start.17
  537.2 6.2 copy-start.23
  543.4 6.1 copy-start.24
  832.0 5.1 copy-start.7
  837.0 3.7 copy-start.6
  840.7 3.7 copy-start.5
  (4 other events, 13.1 us)

commit v4 on v3

--- a/solution.py
+++ b/solution.py
@@ -10,10 +10,11 @@
 CONV_TAPS = 4
 PAD = CONV_TAPS - 1
 SEND_SLOTS = 4
-CHUNK = 64
-LAG_JOIN = 2
-LAG_TOTAL = 5
-LAG_END = 9
+CHUNK = 32
+LAG_JOIN = 3
+LAG_TOTAL = 7
+LAG_END = 12
+DENSE_EVERY = 2
 F32 = jnp.float32
 BF16 = jnp.bfloat16
 MESH = pl.DeviceIdType.MESH
@@ -94,6 +95,10 @@
 
 def head_cols(head):
     return pl.ds(pl.multiple_of(head * HEAD_DIM, HEAD_DIM), HEAD_DIM)
+
+
+def front_lanes(branch, row):
+    return pl.ds((branch * PAD + row) * HEAD_DIM, HEAD_DIM)
 
 
 def head_columns(array_in, n_heads):
@@ -324,7 +329,6 @@
                 d_act = inv_norm * (d_act - unit * jnp.sum(unit * d_act, axis=-1, keepdims=True))
             d_conv = d_act * (sig * (1.0 + conv_sum * (1.0 - sig)))
             dext[branch, pl.ds(0, seq_dev), cols] = d_conv
-            front_send[slot, branch, :, cols] = d_conv[0:8]
             for tap_idx in range(CONV_TAPS):
                 prod = d_conv * ext[branch, pl.ds(8 - PAD + tap_idx, seq_dev), cols]
                 dtaps_ref[branch, tap_idx, :, cols] += jnp.sum(prod.reshape(seq_dev // 8, 8, HEAD_DIM), axis=0)
@@ -332,19 +336,28 @@
 
     lax.fori_loop(0, n_heads, act_head, 0)
 
+    for branch in range(3):
+        for row in range(PAD):
+            for head in range(n_heads):
+                front_send[slot, head:head + 1, front_lanes(branch, row)] = dext[branch, row:row + 1, head * HEAD_DIM:(head + 1) * HEAD_DIM]
+
+    @pl.when(me < groups - 1)
+    def _():
+        front_hop(slot, step).wait_recv()
+
+    for branch in range(3):
+        for row in range(PAD):
+            for head in range(n_heads):
+                dext[branch, seq_dev + row:seq_dev + row + 1, head * HEAD_DIM:(head + 1) * HEAD_DIM] = front[from_next, head:head + 1, front_lanes(branch, row)]
+
     @pl.when(me > 0)
     def _():
         front_hop(slot, step).start()
-
-    @pl.when(me < groups - 1)
-    def _():
-        front_hop(slot, step).wait_recv()
 
     def conv_head(head, carry):
         cols = head_cols(head)
         for branch in range(3):
             taps = taps_ref[branch, :, cols]
-            dext[branch, pl.ds(seq_dev, 8), cols] = front[from_next, branch, :, cols]
             total = dext[branch, pl.ds(PAD, seq_dev), cols] * taps[0:1]
             for tap_idx in range(1, CONV_TAPS):
                 total = total + dext[branch, pl.ds(PAD - tap_idx, seq_dev), cols] * taps[tap_idx:tap_idx + 1]
@@ -417,8 +430,8 @@
         scratch_shapes=[
             pltpu.VMEM((n_seqs, n_heads, HEAD_DIM, HEAD_DIM), F32),
             pltpu.VMEM((SEND_SLOTS, n_heads, HEAD_DIM, HEAD_DIM), F32),
-            pltpu.VMEM((n_seqs, 3, 8, model_dim), F32),
-            pltpu.VMEM((SEND_SLOTS, 3, 8, model_dim), F32),
+            pltpu.VMEM((n_seqs, n_heads, 3 * PAD * HEAD_DIM), F32),
+            pltpu.VMEM((SEND_SLOTS, n_heads, 3 * PAD * HEAD_DIM), F32),
             pltpu.VMEM((3, seq_dev + 8, model_dim), F32),
             pltpu.VMEM((3, seq_dev + 8, model_dim), F32),
             pltpu.VMEM((3, n_heads, seq_dev, HEAD_DIM), BF16),
@@ -520,7 +533,7 @@
             load_copy(idx).wait()
             pair_copy(idx).wait_recv()
 
-    @pl.when(step < n_seqs)
+    @pl.when((step < n_seqs * DENSE_EVERY) & (lax.rem(step, DENSE_EVERY) == 0))
     def _():
         y_ref[0] = lax.dot_general(h_ref[0], wo_ref[...], (((1,), (0,)), ((), ())), preferred_element_type=F32).astype(BF16)
         total = lax.dot_general(dg_ref[0], wg_ref[...], (((1,), (1,)), ((), ())), preferred_element_type=F32)
@@ -586,7 +599,7 @@
     any_spec = pl.BlockSpec(memory_space=pl.ANY)
 
     def row_block(arr):
-        return pl.BlockSpec((1,) + tuple(arr.shape[1:]), lambda step: (jnp.minimum(step, n_seqs - 1), 0, 0))
+        return pl.BlockSpec((1,) + tuple(arr.shape[1:]), lambda step: (jnp.minimum(step // DENSE_EVERY, n_seqs - 1), 0, 0))
 
     outs = [jax.ShapeDtypeStruct(part.shape, F32) for part in parts] + [jax.ShapeDtypeStruct(acts[0].shape, BF16)] * 2
     buf = pltpu.VMEM((n_rows, model_dim), F32)

time: 865 us -> 838 us (0.969)
  Pallas kernels: 744 us -> 716 us
    pallas_call x1, Pallas kernels: 292 us -> 272 us  [run_backward(): pl.pallas_call(functools.partial(backward_kernel, groups), grid=(n_seqs,)...]
where the time goes in v4:
time: 838 us; the launch traced here: 830 us
  Pallas kernels  716 us (85%)
  matrix products  71.7 us (9%)
  local copies, waits for them, and re-layouts  35.2 us (4%)
    pallas_call x1, Pallas kernels, run_backward(): pl.pallas_call(functools.partial(backward_kernel, groups), grid=(n_seqs,)...  272 us
    pallas_call x1, Pallas kernels, run_tail(): pl.pallas_call(functools.partial(tail_kernel, n_seqs), grid=(n_chunks + L...  265 us
    pallas_call x1, Pallas kernels, run_forward(): pl.pallas_call(functools.partial(forward_kernel, groups), grid=(n_seqs,),...  180 us
    dot_general x5, matrix products, weight_grad(): jnp.einsum('btd,bte->de', act_in, grad_in, preferred_element_type=F32)  35.1 us
    unnamed x62, local copies, waits for them, and re-layouts  28.4 us
    dot_general x5, matrix products, project(): return jnp.einsum('btd,de->bte', act_in, weight, preferred_element_type=F32)  27.3 us
  transfers between devices with their start and end apart: 1, of which 0 were waited for; matrix products, arithmetic and copies ran while one was open for 2% of the time, Pallas kernels for 0%

profile of v4, /device:TPU:0, one launch (start us, length us, event | category | flops | bytes accessed | tf_op | source)
XLA Modules:
  0.0 830.4 jit_solution(7705088519002892752)
XLA Ops:
  0.7 7.5 convolution_convert_fusion.4.pq_ref
  8.4 1.9 copy-done.9
  10.2 4.7 convolution_convert_fusion.3.pk_ref
  15.1 4.8 convolution_convert_fusion.2.pv_ref
  20.7 3.0 collective-permute-start
  23.7 6.1 convolution_convert_fusion.1.z_ref
  29.9 6.3 convolution_convert_fusion.dh_ref
  38.2 4.2 convolution_convert_fusion.5.logit_ref
  43.8 180.0 %delta_forward.1 = (bf16[32,64,1024]{2,1,0:T(8,128)(2,1)}, bf16[32,64,1024]{2,1,0:T(8,128)(2,1)}, bf16[32,8,64,128]{3,2,1,0:T(8,128)(2,1)}, bf16[32,8,64,128]{3,...) custom-call(bf16[32,64,1024]{2,1,0:T(8,128)(2,1)} %copy-done.9, ...), custom_call_target="tpu_custom_call" | custom-call | flops 199999995904 | bytes 120000000 | tf_op jit(solution)/shard_map/delta_forward/pallas_call | solution.py:396
  223.8 271.6 %delta_backward.1 = (bf16[32,64,1024]{2,1,0:T(8,128)(2,1)}, bf16[32,64,1024]{2,1,0:T(8,128)(2,1)}, bf16[32,64,1024]{2,1,0:T(8,128)(2,1)}, bf16[32,64,8]{2,1,0:T(8,128)(2,1)}, f32[3,4,8,1024]{3,2,1,0:T(8,128)}) custom-call(bf16[32,64,1024]{2,1,0:T(8,128)(2,1)} %copy-done.9, bf16[32,64,1024]{2,1,0:T(8,128)(2,1)} %copy-done.10, ...), custom_call_target="tpu_custom_call" | custom-call | flops 249999998976 | bytes 120000000 | tf_op jit(solution)/shard_map/delta_backward/pallas_call | solution.py:424
  496.5 3.0 convolution_bitcast_fusion.5
  500.3 10.2 %convolution_bitcast_fusion.refs_4_ = f32[1024,1024]{1,0:T(8,128)} fusion(bf16[32,64,1024]{2,1,0:T(8,128)(2,1)} %get-tuple-element.46.refs_10_, bf16[32,64,1024]{2,1,0:T(8,128)(2,1)} %param.12), kind=kOutput, calls=%fused_computation.5 | convolution fusion | flops 4294967296 | bytes 12582912 | tf_op jit(solution)/shard_map/btd,bte->de/dot_general | solution.py:33
  510.5 6.2 convolution_bitcast_fusion.1.refs_3_
  516.7 6.2 convolution_bitcast_fusion.2.refs_2_
  522.9 6.1 convolution_bitcast_fusion.3.refs_1_
  529.0 6.4 convolution_bitcast_fusion.4.refs_0_
  535.5 264.9 %sum_and_project.1 = (f32[1024,1024]{1,0:T(8,128)}, f32[1024,1024]{1,0:T(8,128)}, f32[1024,1024]{1,0:T(8,128)}, f32[1024,1024]{1,0:T(8,128)}, f32[1024,1024]{1,0...) custom-call(f32[1024,1024]{1,0:T(8,128)} %convolution_bitcast_fusion.4.refs_0_, ...), custom_call_target="tpu_custom_call" | custom-call | flops 249999998976 | bytes 120000000 | tf_op jit(solution)/shard_map/sum_and_project/pallas_call | solution.py:608
  804.4 5.1 copy.58
  809.4 2.1 copy.59
  813.1 2.1 copy.60
  816.8 2.1 copy.61
  820.5 2.1 copy.62
  824.2 2.1 copy.63
  827.9 2.0 copy.64
  (71 shorter events, 18.2 us)
Async XLA Ops:
  0.6 9.6 %copy-start = (bf16[32,64,1024]{2,1,0:T(8,128)(2,1)S(1)}, bf16[32,64,1024]{2,1,0:T(8,128)(2,1)}, u32[]{:S(2)}) copy-start(bf16[32,64,1024]{2,1,0:T(8,128)(2,1)} %param.12) | copy-start | bytes 12582916
  0.7 9.6 %copy-start.18 = (bf16[1024,1024]{1,0:T(8,128)(2,1)S(1)}, bf16[1024,1024]{1,0:T(8,128)(2,1)}, u32[]{:S(2)}) copy-start(bf16[1024,1024]{1,0:T(8,128)(2,1)} %refs_15_.1) | copy-start | bytes 6291460
  10.2 4.9 copy-start.19
  14.9 5.0 copy-start.10
  15.1 8.6 %copy-start.20 = (bf16[1024,1024]{1,0:T(8,128)(2,1)S(1)}, bf16[1024,1024]{1,0:T(8,128)(2,1)}, u32[]{:S(2)}) copy-start(bf16[1024,1024]{1,0:T(8,128)(2,1)} %refs_13_.1) | copy-start | bytes 6291460
  19.9 9.9 %copy-start.11 = (bf16[32,64,1024]{2,1,0:T(8,128)(2,1)}, bf16[32,64,1024]{2,1,0:T(8,128)(2,1)S(1)}, u32[]{:S(2)}) copy-start(bf16[32,64,1024]{2,1,0:T(8,128)(2,1)S(1)} %convolution_convert_fusion.2.pv_ref) | copy-start | bytes 12582916
  20.7 9.2 %copy-start.16 = (bf16[32,64,1024]{2,1,0:T(8,128)(2,1)S(1)}, bf16[32,64,1024]{2,1,0:T(8,128)(2,1)}, u32[]{:S(2)}) copy-start(bf16[32,64,1024]{2,1,0:T(8,128)(2,1)} %param.13) | copy-start | bytes 12582916
  20.7 9.2 %copy-start.21 = (bf16[1024,1024]{1,0:T(8,128)(2,1)S(1)}, bf16[1024,1024]{1,0:T(8,128)(2,1)}, u32[]{:S(2)}) copy-start(bf16[1024,1024]{1,0:T(8,128)(2,1)} %refs_12_.1) | copy-start | bytes 6291460
  20.7 21.7 %collective-permute-start = (bf16[32,3,3072]{2,0,1:T(8,128)(2,1)S(1)}, bf16[32,3,3072]{2,0,1:T(8,128)(2,1)S(1)}, u32[]{:S(2)}, u32[]{:S(2)}) collective-permute-start(bf16[32,3,3072]{2,0,1:T(8,128)(2,1)S(1)} %copy.31), channel_id=1, source_target_pairs={{0,1},{1,2},{2,3},{3,4},{4,5},{5,6},{6,7},{8,9},{9,10},{10,11},{11... | collective-permute-start | bytes 1769480 | tf_op jit(solution)/shard_map/ppermute | solution.py:631
  29.8 6.3 copy-start.12
  29.8 6.3 copy-start.13
  29.9 6.3 copy-start.14
  29.9 6.9 copy-start.8
  29.9 7.8 copy-start.22
  495.4 4.2 copy-start.15
  500.3 10.2 %copy-start.1 = (bf16[32,64,1024]{2,1,0:T(8,128)(2,1)S(1)}, bf16[32,64,1024]{2,1,0:T(8,128)(2,1)}, u32[]{:S(2)}) copy-start(bf16[32,64,1024]{2,1,0:T(8,128)(2,1)} %param.12) | copy-start | bytes 12582916
  500.3 10.2 %copy-start.26 = (bf16[32,64,1024]{2,1,0:T(8,128)(2,1)S(1)}, bf16[32,64,1024]{2,1,0:T(8,128)(2,1)}, u32[]{:S(2)}) copy-start(bf16[32,64,1024]{2,1,0:T(8,128)(2,1)} %get-tuple-element.45.refs_9_) | copy-start | bytes 12582916
  510.5 6.2 copy-start.25
  516.7 6.2 copy-start.17
  516.7 6.2 copy-start.23
  522.9 6.1 copy-start.24
  804.4 5.1 copy-start.7
  809.4 3.7 copy-start.6
  816.8 3.7 copy-start.4
  (4 other events, 13.1 us)
